TPU v7x, 32 devices: a whole 2x2x4 slice. The times are simulated.
32 devices in a mesh: mem: 8 (over z, x), grid: 4 (over y, core).
Axes of the slice: x: 2, y: 2, z: 4, core: 2. Of those that a mesh axis runs over, the one named last changes fastest.
Arguments:
- alpha: bfloat16 [16, 8, 768, 1536], P('mem', None, 'grid'), may hold values from -6 to 6
- perturbation: bfloat16 [16, 8, 768, 1536], P('mem', None, 'grid'), may hold values from -6 to 6
- legendre: bfloat16 [192, 128, 768], P('grid'), may hold values from -0.21875 to 0.21875
- response: float32 [192, 128], P('grid'), may hold values from 0.2 to 2
Outputs:
- increment: float32 [8, 768, 1536], P('mem', 'grid')
All inputs are finite; a program needn't handle non-finite values.
Results may differ from a plain program's by a relative error of at most 0.0063.
Values may be sent and summed in bfloat16 or wider, within the bound.
A program may use at most 128 MiB of HBM per device.

v0:
```python
import math

import jax
import jax.numpy as jnp
from jax import lax
from jax.sharding import PartitionSpec as P


def build_tables(lon_count, keep_dev, grid_count):
    col = jnp.arange(2 * keep_dev * grid_count, dtype=jnp.int32)
    block = col // (2 * keep_dev)
    part = col // keep_dev % 2
    wave = block * keep_dev + col % keep_dev
    lon = jnp.arange(lon_count, dtype=jnp.int32)
    phase = lon[:, None] * wave[None, :] % lon_count
    angle = phase.astype(jnp.float32) * jnp.float32(2.0 * math.pi / lon_count)
    basis = jnp.where(part[None, :] == 0, jnp.cos(angle), jnp.sin(angle))
    weight = jnp.where(wave == 0, jnp.float32(1.0), jnp.float32(2.0)) / jnp.float32(lon_count)
    forward = basis.astype(jnp.bfloat16)
    inverse = jnp.transpose(basis * weight[None, :]).astype(jnp.bfloat16)
    return (forward, inverse)


def legendre_filter(piece, legendre, response):
    cols, mem_dev, items, lat_count = piece.shape
    keep_dev = legendre.shape[0]
    split = piece.reshape(2, keep_dev, mem_dev, items, lat_count)
    coef = jnp.einsum("mnt,qmkit->qmkin", legendre, split, preferred_element_type=jnp.float32)
    coef = (coef * response[None, :, None, None, :]).astype(jnp.bfloat16)
    synth = jnp.einsum("mnt,qmkin->qmkit", legendre, coef, preferred_element_type=jnp.float32)
    return synth.astype(jnp.bfloat16).reshape(cols, mem_dev, items, lat_count)


def body(alpha, perturbation, legendre, response):
    mem_dev, levels, lat_dev, lon_count = alpha.shape
    keep_dev = legendre.shape[0]
    grid_count = lax.axis_size("grid")
    mem_count = lax.axis_size("mem")
    members = mem_dev * mem_count
    forward, inverse = build_tables(lon_count, keep_dev, grid_count)
    spectra = jnp.einsum("xc,klyx->ckly", forward, alpha, preferred_element_type=jnp.float32)
    spectra = spectra.astype(jnp.bfloat16)
    filtered = legendre_filter(
        lax.all_to_all(spectra, "grid", split_axis=0, concat_axis=3, tiled=True), legendre, response
    )
    returned = lax.all_to_all(filtered, "grid", split_axis=3, concat_axis=0, tiled=True)
    values = jnp.einsum("ckly,cx->klyx", returned, inverse, preferred_element_type=jnp.float32)
    total = lax.psum_scatter(
        jnp.sum(values * perturbation, axis=0), "mem", scatter_dimension=0, tiled=True
    )
    return total / jnp.sqrt(jnp.float32(members - 1))


def solution(mesh):
    placed = (
        P("mem", None, "grid", None),
        P("mem", None, "grid", None),
        P("grid", None, None),
        P("grid", None),
    )
    return jax.shard_map(
        body, mesh=mesh, in_specs=placed, out_specs=P("mem", "grid", None), check_vma=False
    )
```

profile of v0, /device:TPU:0, one launch (start us, length us, event | category | flops | bytes accessed | tf_op | source)
XLA Modules:
  0.0 337.0 jit_solution(17224794517558854112)
XLA Ops:
  6.6 17.5 %convolution_convert_fusion = bf16[384,2,8,192]{0,3,2,1:T(8,128)(2,1)} fusion(bf16[2,8,192,1536]{3,2,1,0:T(8,128)(2,1)} %param.4, s32[384]{0:T(512)S(1)} %fusion.57, pred[384]{0:T(512)(128)(4,1)S(1)} %fusion.59), kind=kOutput, calls=%fused_computation.25 | convolution fusion | flops 3631546368 | bytes 11798400 | tf_op jit(solution)/shard_map/xc,klyx->ckly/dot_general | solution.py:41
  24.1 4.0 %copy.15 = bf16[384,2,8,192]{3,2,1,0:T(8,128)(2,1)S(1)} copy(bf16[384,2,8,192]{0,3,2,1:T(8,128)(2,1)} %convolution_convert_fusion) | data formatting | bytes 4718592 | tf_op jit(solution)/shard_map/convert_element_type | solution.py:42
  28.1 41.0 %all_to_all.33 = bf16[384,2,8,192]{3,2,1,0:T(8,128)(2,1)S(1)} all-to-all(bf16[384,2,8,192]{3,2,1,0:T(8,128)(2,1)S(1)} %copy.15), channel_id=1, replica_groups=mesh['mem'=8,'grid'=4] {'grid'}, dimensions={0} | all-to-all | bytes 4718592 | tf_op jit(solution)/shard_map/all_to_all | solution.py:44
  69.1 4.0 %copy.40 = bf16[4,96,2,8,192]{4,0,3,2,1:T(4,128)(2,1)S(1)} copy(bf16[4,96,2,8,192]{4,3,2,1,0:T(8,128)(2,1)S(1)} %bitcast.48) | data formatting | bytes 4718592 | tf_op jit(solution)/shard_map/all_to_all | solution.py:44
  73.1 0.0 copy-start
  73.1 3.8 %reshape.57 = bf16[2,48,2,8,768]{4,3,2,1,0:T(8,128)(2,1)} reshape(bf16[96,2,8,4,192]{4,3,2,1,0:T(4,128)(2,1)S(1)} %bitcast.49) | data formatting | bytes 4718592 | tf_op jit(solution)/shard_map/reshape | solution.py:27
  76.9 0.0 copy-done
  76.9 11.5 %convert_bitcast_fusion = bf16[2,48,2,8,768]{4,3,2,0,1:T(8,128)(2,1)S(1)} fusion(bf16[48,128,768]{2,1,0:T(8,128)(2,1)} %param.6, bf16[2,48,2,8,768]{4,3,2,1,0:T(8,128)(2,1)} %reshape.57, f32[48,128]{1,0:T(8,128)S(1)} %copy-done), kind=kOutput, calls=%fused_computation.18 | convolution fusion | flops 605552640 | bytes 14180352 | tf_op jit(solution)/shard_map/mnt,qmkin->qmkit/dot_general | solution.py:30
  88.4 1.6 copy.18
  90.1 5.3 %copy.19 = bf16[96,2,8,768]{0,2,1,3:T(8,128)(2,1)} copy(bf16[96,2,8,768]{3,2,1,0:T(8,128)(2,1)} %bitcast.51) | data formatting | bytes 4718592 | tf_op jit(solution)/shard_map/reshape | solution.py:31
  95.4 3.7 %all-to-all-start.1 = ((bf16[96,2,8,768]{0,2,1,3:T(8,128)(2,1)}), bf16[96,2,8,768]{0,2,1,3:T(8,128)(2,1)S(1)}, u32[]{:S(2)}, u32[]{:S(2)}) async-start(bf16[96,2,8,768]{0,2,1,3:T(8,128)(2,1)} %copy.19), calls=%async_computation.1 | async-start | bytes 6291456 | tf_op jit(solution)/shard_map/all_to_all | solution.py:46
  99.1 0.3 reduce-scatter.2.cloned.1.call-start
  99.4 36.6 %all-to-all-done.1 = bf16[96,2,8,768]{0,2,1,3:T(8,128)(2,1)S(1)} async-done(((bf16[96,2,8,768]{0,2,1,3:T(8,128)(2,1)}), bf16[96,2,8,768]{0,2,1,3:T(8,128)(2,1)S(1)}, u32[]{:S(2)}, u32[]{:S(2)}) %all-to-all-start.1) | async-done | bytes 2359328 | tf_op jit(solution)/shard_map/all_to_all | solution.py:46
  135.9 4.1 %copy.39 = bf16[96,2,8,4,192]{0,3,4,2,1:T(4,128)(2,1)} copy(bf16[96,2,8,4,192]{0,2,1,4,3:T(8,128)(2,1)S(1)} %bitcast.47) | data formatting | bytes 4718592 | tf_op jit(solution)/shard_map/all_to_all | solution.py:46
  140.0 5.0 %all_to_all.30 = bf16[384,2,8,192]{0,3,2,1:T(8,128)(2,1)S(1)} reshape(bf16[4,96,2,8,192]{1,0,4,3,2:T(4,128)(2,1)} %bitcast.50) | data formatting | bytes 4718592 | tf_op jit(solution)/shard_map/all_to_all | solution.py:46
  145.0 20.1 %multiply_reduce_fusion = f32[8,192,1536]{2,1,0:T(8,128)} fusion(bf16[2,8,192,1536]{3,2,1,0:T(8,128)(2,1)} %param.5, bf16[384,2,8,192]{0,3,2,1:T(8,128)(2,1)S(1)} %all_to_all.30, f32[384]{0:T(512)S(1)} %select_multiply_fusion, s32[384]{0:T(512)S(1)} %fusion.57, pred[384]{0:T(512)(128)(4,1)S(1)} %fusion.59), kind=kOutput, calls=%fused_computation | convolution fusion | flops 3642753024 | bytes 21237120 | tf_op jit(solution)/shard_map/ckly,cx->klyx/dot_general | solution.py:47
  165.1 0.0 reduce-scatter.2.cloned.1.call-update
  165.2 162.6 %reduce-scatter.2.cloned.1.call-done = f32[1,192,1536]{2,1,0:T(8,128)} async-done(((f32[8,192,1536]{2,1,0:T(8,128)}), f32[1,192,1536]{2,1,0:T(8,128)}) %reduce-scatter.2.cloned.1.call-update) | async-done | bytes 1179664 | tf_op jit(solution)/shard_map/reduce_scatter | solution.py:48
  327.7 2.4 broadcast_multiply_fusion
  (3 shorter events, 0.0 us)
Async XLA Ops:
  73.1 3.8 %copy-start = (f32[48,128]{1,0:T(8,128)S(1)}, f32[48,128]{1,0:T(8,128)}, u32[]{:S(2)}) copy-start(f32[48,128]{1,0:T(8,128)} %param.7) | copy-start | bytes 73732
  95.4 40.6 %all-to-all-start.1 = ((bf16[96,2,8,768]{0,2,1,3:T(8,128)(2,1)}), bf16[96,2,8,768]{0,2,1,3:T(8,128)(2,1)S(1)}, u32[]{:S(2)}, u32[]{:S(2)}) async-start(bf16[96,2,8,768]{0,2,1,3:T(8,128)(2,1)} %copy.19), calls=%async_computation.1 | async-start | bytes 6291456 | tf_op jit(solution)/shard_map/all_to_all | solution.py:46
  99.1 228.7 %reduce-scatter.2.cloned.1.call-start = ((), (), s32[]{:S(2)}) async-start(), calls=%async_computation.3 | async-start | bytes 10616832 | tf_op jit(solution)/shard_map/reduce_scatter | solution.py:48
Sparse Core Ops, SparseCore 0:
  165.3 162.3 reduce-scatter.1
where the time goes:
time: 337 us
  waiting for transfers between devices  199 us (59%)
  matrix products  49.2 us (15%)
  blocking collectives  41 us (12%)
  local copies, waits for them, and re-layouts  27.8 us (8%)
  between operations  13.5 us (4%)
  starting transfers between devices  3.96 us (1%)
    reduce_scatter x1, waiting for transfers between devices, body(): lax.psum_scatter(jnp.sum(values * perturbation, axis=0), 'mem', scatter_d...  163 us
    all_to_all x1, blocking collectives, body(): lax.all_to_all(spectra, 'grid', split_axis=0, concat_axis=3, tiled=True)  41 us
    all_to_all x1, waiting for transfers between devices, body(): lax.all_to_all(filtered, 'grid', split_axis=3, concat_axis=0, tiled=True)  36.6 us
    dot_general x1, matrix products, body(): jnp.einsum('ckly,cx->klyx', returned, inverse, preferred_element_type=jnp...  20.1 us
    dot_general x1, matrix products, body(): jnp.einsum('xc,klyx->ckly', forward, alpha, preferred_element_type=jnp.fl...  17.5 us
    dot_general x1, matrix products, legendre_filter(): jnp.einsum('mnt,qmkin->qmkit', legendre, coef, preferred_element_type=jnp...  11.5 us
    all_to_all x2, local copies, waits for them, and re-layouts, body(): lax.all_to_all(filtered, 'grid', split_axis=3, concat_axis=0, tiled=True)  9.05 us
  transfers between devices with their start and end apart: 2, of which 2 were waited for; matrix products, arithmetic and copies ran while one was open for 0% of the time, Pallas kernels for 0%

commit v1 on v0

v1 whole, which is shorter than its diff:
```python
import functools
import math

import jax
import jax.numpy as jnp
import numpy as np
from jax import lax
from jax.experimental import pallas as pl
from jax.experimental.pallas import tpu as pltpu
from jax.sharding import PartitionSpec as P


def build_table(lon_count, keep_dev, grid_count):
    col = np.arange(2 * keep_dev * grid_count)
    block = col // (2 * keep_dev)
    part = col // keep_dev % 2
    wave = block * keep_dev + col % keep_dev
    phase = wave[:, None] * np.arange(lon_count)[None, :] % lon_count
    angle = phase.astype(np.float32) * np.float32(2.0 * math.pi / lon_count)
    basis = np.where(part[:, None] == 0, np.cos(angle), np.sin(angle))
    return jnp.asarray(basis.astype(jnp.bfloat16))


def legendre_filter(split, legendre, response):
    coef = jnp.einsum("mnt,qmkit->qmkin", legendre, split, preferred_element_type=jnp.float32)
    coef = (coef * response[None, :, None, None, :]).astype(jnp.bfloat16)
    synth = jnp.einsum("mnt,qmkin->qmkit", legendre, coef, preferred_element_type=jnp.float32)
    return synth.astype(jnp.bfloat16)


def reduce_levels(partial, levels):
    mem_count = lax.axis_size("mem")
    me = lax.axis_index("mem")
    owned = levels // mem_count
    if mem_count % 2:
        every = jnp.concatenate([partial(i * owned, owned) for i in range(mem_count)])
        return lax.psum_scatter(every, "mem", scatter_dimension=0, tiled=True)
    ring = mem_count // 2
    side, place = me % 2, me // 2
    swap = [(j, j ^ 1) for j in range(mem_count)]
    onward = [(j, (j + 2) % mem_count) for j in range(mem_count)]
    total = None
    for step in range(ring):
        goal = (place + 2 * ring - 1 - step) % ring
        give = partial((2 * goal + 1 - side) * owned, owned).astype(jnp.bfloat16)
        got = lax.ppermute(give, "mem", swap)
        here = partial((2 * goal + side) * owned, owned)
        here = here + got.astype(jnp.float32)
        if total is not None:
            here = here + total.astype(jnp.float32)
        if step < ring - 1:
            total = lax.ppermute(here.astype(jnp.bfloat16), "mem", onward)
    return here


def filter_kernel(lat_dev, x_ref, legendre_ref, response_ref, out_ref, rows_ref, back_ref):
    grid_count, parts, waves, points = x_ref.shape
    tiles = points // 128
    per_pair = 2 * lat_dev // 128
    pairs = tiles // per_pair
    half = per_pair // 2
    for src in range(grid_count):
        for part in range(parts):
            for tile in range(tiles):
                spot = (tile % per_pair) * pairs + tile // per_pair
                rows_ref[src, part, spot * waves : (spot + 1) * waves, :] = x_ref[
                    src, part, :, tile * 128 : (tile + 1) * 128
                ].astype(jnp.float32)

    def one_wave(wave, carry):
        lines = []
        for part in range(parts):
            even, odd = [], []
            for src in range(grid_count):
                block = rows_ref[src, part, pl.ds(wave, tiles, stride=waves), :]
                piece = [block[i * pairs : (i + 1) * pairs] for i in range(per_pair)]
                even += piece[:half] + [piece[half][:, :64]]
                odd += [piece[half][:, 64:]] + piece[half + 1 :]
            lines += [jnp.concatenate(even, axis=1), jnp.concatenate(odd, axis=1)]
        field = jnp.concatenate(lines, axis=0).astype(jnp.bfloat16)
        basis = legendre_ref[wave]
        coef = lax.dot_general(
            field, basis, (((1,), (1,)), ((), ())), preferred_element_type=jnp.float32
        )
        coef = (coef * response_ref[pl.ds(wave, 1), :]).astype(jnp.bfloat16)
        synth = jnp.dot(coef, basis, preferred_element_type=jnp.float32)
        for part in range(parts):
            even = synth[2 * part * pairs : (2 * part + 1) * pairs]
            odd = synth[(2 * part + 1) * pairs : (2 * part + 2) * pairs]
            for src in range(grid_count):
                base = src * lat_dev
                both = jnp.concatenate(
                    [even[:, base : base + lat_dev], odd[:, base : base + lat_dev]], axis=1
                )
                block = jnp.concatenate(
                    [both[:, i * 128 : (i + 1) * 128] for i in range(per_pair)], axis=0
                )
                back_ref[src, part, pl.ds(wave, tiles, stride=waves), :] = block
        return carry

    lax.fori_loop(0, waves, one_wave, 0)
    for src in range(grid_count):
        for part in range(parts):
            for tile in range(tiles):
                spot = (tile % per_pair) * pairs + tile // per_pair
                out_ref[src, part, :, tile * 128 : (tile + 1) * 128] = back_ref[
                    src, part, spot * waves : (spot + 1) * waves, :
                ].astype(jnp.bfloat16)


def filter_packed(spectra, legendre, response, lat_dev, start, count):
    grid_count, parts, _, points = spectra.shape
    degrees, lat_count = legendre.shape[1:]
    waves = 16
    first = start // waves
    block = pl.BlockSpec((grid_count, parts, waves, points), lambda i: (0, 0, i, 0))
    return pl.pallas_call(
        functools.partial(filter_kernel, lat_dev),
        out_shape=jax.ShapeDtypeStruct(spectra.shape, jnp.bfloat16),
        grid=(count // waves,),
        in_specs=[
            block,
            pl.BlockSpec((waves, degrees, lat_count), lambda i: (i + first, 0, 0)),
            pl.BlockSpec((waves, degrees), lambda i: (i + first, 0)),
        ],
        out_specs=block,
        scratch_shapes=[
            pltpu.VMEM((grid_count, parts, points // 128 * waves, 128), jnp.float32),
            pltpu.VMEM((grid_count, parts, points // 128 * waves, 128), jnp.float32),
        ],
        compiler_params=pltpu.CompilerParams(vmem_limit_bytes=40 * 2**20),
        cost_estimate=pl.CostEstimate(
            flops=8 * count * degrees * lat_count * points // lat_dev,
            bytes_accessed=2 * count * degrees * lat_count,
            transcendentals=0,
        ),
    )(spectra, legendre, response)


def synth_kernel(where_ref, field_ref, table_ref, weight_ref, give_ref, keep_ref, total_ref):
    member = pl.program_id(1)
    side = where_ref[1]
    pair, lat_dev, wide = total_ref.shape
    values = lax.dot_general(
        field_ref[...], table_ref[...], (((0,), (0,)), ((), ())), preferred_element_type=jnp.float32
    ).reshape(pair, lat_dev, wide)
    term = values * weight_ref[0].astype(jnp.float32)

    @pl.when(member == 0)
    def _():
        total_ref[...] = term

    @pl.when(member > 0)
    def _():
        total_ref[...] += term

    @pl.when(member == pl.num_programs(1) - 1)
    def _():
        give_ref[0] = total_ref[1 - side].astype(jnp.bfloat16)
        keep_ref[0] = total_ref[side]


def synth_pair(filtered, table, perturbation, goal, side):
    mem_dev, levels, lat_dev, lon_count = perturbation.shape
    cols = table.shape[0]
    pairs = levels // 2
    wide = math.gcd(lon_count, 512)
    level = pl.BlockSpec((1, lat_dev, wide), lambda i, k, w: (0, 0, i))
    return pl.pallas_call(
        synth_kernel,
        out_shape=(
            jax.ShapeDtypeStruct((1, lat_dev, lon_count), jnp.bfloat16),
            jax.ShapeDtypeStruct((1, lat_dev, lon_count), jnp.float32),
        ),
        grid_spec=pltpu.PrefetchScalarGridSpec(
            num_scalar_prefetch=1,
            grid=(lon_count // wide, mem_dev),
            in_specs=[
                pl.BlockSpec((cols, 2 * lat_dev), lambda i, k, w: (0, k * pairs + w[0])),
                pl.BlockSpec((cols, wide), lambda i, k, w: (0, i)),
                pl.BlockSpec((1, 2, lat_dev, wide), lambda i, k, w: (k, w[0], 0, i)),
            ],
            out_specs=(level, level),
            scratch_shapes=[pltpu.VMEM((2, lat_dev, wide), jnp.float32)],
        ),
        compiler_params=pltpu.CompilerParams(vmem_limit_bytes=24 * 2**20),
        cost_estimate=pl.CostEstimate(
            flops=4 * mem_dev * lat_dev * cols * lon_count,
            bytes_accessed=4 * mem_dev * lat_dev * lon_count,
            transcendentals=0,
        ),
    )(jnp.stack([goal, side]).astype(jnp.int32), filtered, table, perturbation)


def reduce_pairs(both):
    mem_count = lax.axis_size("mem")
    me = lax.axis_index("mem")
    ring = mem_count // 2
    side, place = me % 2, me // 2
    swap = [(j, j ^ 1) for j in range(mem_count)]
    onward = [(j, (j + 2) % mem_count) for j in range(mem_count)]
    total = None
    for step in range(ring):
        goal = (place + 2 * ring - 1 - step) % ring
        give, here = both(goal, side)
        here = here + lax.ppermute(give, "mem", swap).astype(jnp.float32)
        if total is not None:
            here = here + total.astype(jnp.float32)
        if step < ring - 1:
            total = lax.ppermute(here.astype(jnp.bfloat16), "mem", onward)
    return here


def packed(alpha, perturbation, legendre, response, table):
    mem_dev, levels, lat_dev, lon_count = alpha.shape
    keep_dev = legendre.shape[0]
    grid_count = lax.axis_size("grid")
    points = mem_dev * levels * lat_dev
    spectra = lax.dot_general(
        table, alpha.reshape(points, lon_count), (((1,), (1,)), ((), ())), preferred_element_type=jnp.float32
    ).astype(jnp.bfloat16)
    spectra = spectra.reshape(grid_count, 2, keep_dev, points)
    chunks = CHUNKS
    step = keep_dev // chunks
    pieces = []
    for i in range(chunks):
        piece = spectra[:, :, i * step : (i + 1) * step].reshape(grid_count, 2 * step, points)
        piece = lax.all_to_all(piece, "grid", split_axis=0, concat_axis=0, tiled=True)
        piece = piece.reshape(grid_count, 2, step, points)
        piece = filter_packed(piece, legendre, response, lat_dev, i * step, step)
        piece = piece.reshape(grid_count, 2 * step, points)
        piece = lax.all_to_all(piece, "grid", split_axis=0, concat_axis=0, tiled=True)
        pieces.append(piece.reshape(grid_count, 2, step, points))
    filtered = jnp.concatenate(pieces, axis=2).reshape(grid_count * 2 * keep_dev, points)
    return reduce_pairs(lambda goal, side: synth_pair(filtered, table, perturbation, goal, side))


CHUNKS = 1


def body(alpha, perturbation, legendre, response):
    mem_dev, levels, lat_dev, lon_count = alpha.shape
    keep_dev = legendre.shape[0]
    grid_count = lax.axis_size("grid")
    members = mem_dev * lax.axis_size("mem")
    cols = 2 * keep_dev
    table = build_table(lon_count, keep_dev, grid_count)
    wave = lax.axis_index("grid") * keep_dev + jnp.arange(keep_dev)
    response = response * jnp.where(wave == 0, 1.0, 2.0).astype(jnp.float32)[:, None]

    scale = jnp.float32(1.0 / (lon_count * math.sqrt(members - 1)))
    if keep_dev % 16 == 0 and lat_dev % 128 == 64 and levels == lax.axis_size("mem") and levels % 2 == 0:
        return packed(alpha, perturbation, legendre, response, table) * scale

    points = mem_dev * levels * lat_dev
    lane = math.gcd(points, 128)
    spectra = jnp.einsum("cx,klyx->ckly", table, alpha, preferred_element_type=jnp.float32)
    spectra = spectra.astype(jnp.bfloat16).reshape(grid_count, cols, points // lane, lane)
    spectra = lax.all_to_all(spectra, "grid", split_axis=0, concat_axis=0, tiled=True)
    split = spectra.reshape(grid_count, 2, keep_dev, mem_dev, levels, lat_dev)
    split = jnp.transpose(split, (1, 2, 3, 4, 0, 5)).reshape(2, keep_dev, mem_dev, levels, -1)
    filtered = legendre_filter(split, legendre, response)
    filtered = filtered.reshape(2, keep_dev, mem_dev, levels, grid_count, lat_dev)
    filtered = jnp.transpose(filtered, (4, 0, 1, 2, 3, 5)).reshape(grid_count, cols, points // lane, lane)
    filtered = lax.all_to_all(filtered, "grid", split_axis=0, concat_axis=0, tiled=True)
    filtered = filtered.reshape(grid_count * cols, mem_dev, levels, lat_dev)
    filtered = jnp.transpose(filtered, (1, 2, 3, 0))

    def partial(level, count):
        field = lax.dynamic_slice_in_dim(filtered, level, count, 1)
        weight = lax.dynamic_slice_in_dim(perturbation, level, count, 1)
        values = jnp.einsum("klyc,cx->klyx", field, table, preferred_element_type=jnp.float32)
        return jnp.sum(values * weight, axis=0)

    total = reduce_levels(partial, levels)
    return total * scale


def solution(mesh):
    placed = (
        P("mem", None, "grid", None),
        P("mem", None, "grid", None),
        P("grid", None, None),
        P("grid", None),
    )
    return jax.shard_map(
        body, mesh=mesh, in_specs=placed, out_specs=P("mem", "grid", None), check_vma=False
    )
```

time: 337 us -> 174 us (0.52)
  waiting for transfers between devices: 199 us -> 86.6 us
  Pallas kernels: 0 us -> 41.1 us
  blocking collectives: 41 us -> 0 us
  matrix products: 49.2 us -> 9.33 us
  between operations: 13.5 us -> 0.15 us
  starting transfers between devices: 3.96 us -> 15.8 us
  local copies, waits for them, and re-layouts: 27.8 us -> 16.2 us
    reduce_scatter x1 -> x0, waiting for transfers between devices: 163 us -> none  [body(): lax.psum_scatter(jnp.sum(values * perturbation, axis=0), 'mem', scatter_d...]
    pallas_call x0 -> x5, Pallas kernels: none -> 41.1 us  [the longest x1 23.5 us: filter_packed(): pl.pallas_call(functools.partial(filter_kernel, lat_dev), out_shape=jax.S...]
    all_to_all x1 -> x0, blocking collectives: 41 us -> none  [body(): lax.all_to_all(spectra, 'grid', split_axis=0, concat_axis=3, tiled=True)]
    dot_general x3 -> x1, matrix products: 49.2 us -> 9.33 us  [packed(): lax.dot_general(table, alpha.reshape(points, lon_count), (((1,), (1,)), (...]
    ppermute x0 -> x7, waiting for transfers between devices: none -> 29.8 us  [the longest x3 15.6 us: reduce_pairs(): total = lax.ppermute(here.astype(jnp.bfloat16), 'mem', onward)]
    all_to_all x1 -> x2, waiting for transfers between devices: 36.6 us -> 56.7 us  [packed(): lax.all_to_all(piece, 'grid', split_axis=0, concat_axis=0, tiled=True)]
    unnamed x2 -> x18, local copies, waits for them, and re-layouts: 0.01 us -> 16.2 us
    all_to_all x3 -> x0, local copies, waits for them, and re-layouts: 13.1 us -> none  [the longest x2 9.05 us: body(): lax.all_to_all(filtered, 'grid', split_axis=3, concat_axis=0, tiled=True)]
  transfers between devices with their start and end apart: 2 -> 9, of which waited for: 2 -> 8; matrix products, arithmetic and copies ran while one was open for 0% -> 2% of each run, Pallas kernels for 0% -> 8%
where the time goes in v1:
time: 174 us; the launch traced here: 173 us
  waiting for transfers between devices  86.6 us (50%)
  Pallas kernels  41.1 us (24%)
  local copies, waits for them, and re-layouts  16.2 us (9%)
  starting transfers between devices  15.8 us (9%)
  matrix products  9.33 us (5%)
  other arithmetic  4.04 us (2%)
    all_to_all x2, waiting for transfers between devices, packed(): lax.all_to_all(piece, 'grid', split_axis=0, concat_axis=0, tiled=True)  56.7 us
    pallas_call x1, Pallas kernels, filter_packed(): pl.pallas_call(functools.partial(filter_kernel, lat_dev), out_shape=jax.S...  23.5 us
    pallas_call x4, Pallas kernels, synth_pair(): pl.pallas_call(synth_kernel, out_shape=(jax.ShapeDtypeStruct((1, lat_dev,...  17.6 us
    unnamed x18, local copies, waits for them, and re-layouts  16.2 us
    ppermute x3, waiting for transfers between devices, reduce_pairs(): total = lax.ppermute(here.astype(jnp.bfloat16), 'mem', onward)  15.6 us
    ppermute x4, waiting for transfers between devices, reduce_pairs(): here = here + lax.ppermute(give, 'mem', swap).astype(jnp.float32)  14.3 us
    dot_general x1, matrix products, packed(): lax.dot_general(table, alpha.reshape(points, lon_count), (((1,), (1,)), (...  9.33 us
    all_to_all x2, starting transfers between devices, packed(): lax.all_to_all(piece, 'grid', split_axis=0, concat_axis=0, tiled=True)  8.15 us
  transfers between devices with their start and end apart: 9, of which 8 were waited for; matrix products, arithmetic and copies ran while one was open for 2% of the time, Pallas kernels for 8%

profile of v1, /device:TPU:0, one launch (start us, length us, event | category | flops | bytes accessed | tf_op | source)
XLA Modules:
  0.0 173.2 jit_solution(14313837827294606349)
XLA Ops:
  0.0 9.3 %convolution_convert_fusion = bf16[384,3072]{1,0:T(8,128)(2,1)} fusion(bf16[384,1536]{1,0:T(8,128)(2,1)} %constant.80.clone.table_ref, bf16[3072,1536]{1,0:T(8,128)(2,1)} %bitcast.19), kind=kOutput, calls=%fused_computation | convolution fusion | flops 3625058304 | bytes 12976128 | tf_op jit(solution)/shard_map/dot_general | solution.py:219
  9.3 4.4 %all-to-all-start = ((bf16[4,96,3072]{2,1,0:T(8,128)(2,1)}), bf16[4,96,3072]{2,1,0:T(8,128)(2,1)S(1)}, u32[]{:S(2)}, u32[]{:S(2)}) async-start(bf16[4,96,3072]{2,1,0:T(8,128)(2,1)} %bitcast.18), calls=%async_computation | async-start | bytes 4718592 | tf_op jit(solution)/shard_map/all_to_all | solution.py:228
  13.7 0.1 broadcast_multiply_fusion.response_ref
  13.8 28.4 %all-to-all-done = bf16[4,96,3072]{2,1,0:T(8,128)(2,1)S(1)} async-done(((bf16[4,96,3072]{2,1,0:T(8,128)(2,1)}), bf16[4,96,3072]{2,1,0:T(8,128)(2,1)S(1)}, u32[]{:S(2)}, u32[]{:S(2)}) %all-to-all-start) | async-done | bytes 2359328 | tf_op jit(solution)/shard_map/all_to_all | solution.py:228
  42.2 3.7 %copy-done.4 = bf16[48,128,768]{2,1,0:T(8,128)(2,1)S(1)} copy-done((bf16[48,128,768]{2,1,0:T(8,128)(2,1)S(1)}, bf16[48,128,768]{2,1,0:T(8,128)(2,1)}, u32[]{:S(2)}) %copy-start.4) | copy-done | bytes 9437208
  45.9 23.5 %shard_map.55 = bf16[4,2,48,3072]{3,2,1,0:T(8,128)(2,1)S(1)} custom-call(bf16[4,2,48,3072]{3,2,1,0:T(8,128)(2,1)S(1)} %bitcast.17, bf16[48,128,768]{2,1,0:T(8,128)(2,1)S(1)} %copy-done.4, f32[48,128]{1,0:T(8,128)S(1)} %broadcast_multiply_fusion.response_ref), custom_call_target="tpu_custom_call" | custom-call | flops 603979776 | bytes 9437184 | tf_op jit(solution)/shard_map/pallas_call | solution.py:117
  69.5 1.4 copy-done.5
  70.9 3.8 %all-to-all-start.1 = ((bf16[4,96,3072]{2,1,0:T(8,128)(2,1)}), bf16[4,96,3072]{2,1,0:T(8,128)(2,1)S(1)}, u32[]{:S(2)}, u32[]{:S(2)}) async-start(bf16[4,96,3072]{2,1,0:T(8,128)(2,1)} %bitcast.16), calls=%async_computation.1 | async-start | bytes 4718592 | tf_op jit(solution)/shard_map/all_to_all | solution.py:232
  74.7 0.1 pad_add_fusion.2
  74.8 28.3 %all-to-all-done.1 = bf16[4,96,3072]{2,1,0:T(8,128)(2,1)S(1)} async-done(((bf16[4,96,3072]{2,1,0:T(8,128)(2,1)}), bf16[4,96,3072]{2,1,0:T(8,128)(2,1)S(1)}, u32[]{:S(2)}, u32[]{:S(2)}) %all-to-all-start.1) | async-done | bytes 2359328 | tf_op jit(solution)/shard_map/all_to_all | solution.py:232
  103.1 3.7 %copy-done = bf16[2,8,192,1536]{3,2,1,0:T(8,128)(2,1)S(1)} copy-done((bf16[2,8,192,1536]{3,2,1,0:T(8,128)(2,1)S(1)}, bf16[2,8,192,1536]{3,2,1,0:T(8,128)(2,1)}, u32[]{:S(2)}) %copy-start) | copy-done | bytes 9437208
  106.8 4.2 %shard_map.59 = (bf16[1,192,1536]{2,1,0:T(8,128)(2,1)S(1)}, f32[1,192,1536]{2,1,0:T(8,128)S(1)}) custom-call(s32[2]{0:T(128)S(1)} %get-tuple-element.24.where_ref, bf16[384,3072]{1,0:T(8,128)(2,1)S(1)} %bitcast.12, bf16[384,1536]{1,0:T(8,128)(2,1)S(1)} %copy-done.3, bf16[2,8,192,1536]{3,2,1,0:T(8,128)(2,1)S(1)} %copy-done), custom_call_target="tpu_custom_call" | custom-call | flops 905969664 | bytes 2359296 | tf_op jit(solution)/shard_map/pallas_call | solution.py:169
  111.0 2.3 %collective-permute-start.3 = (bf16[1,192,1536]{2,1,0:T(8,128)(2,1)S(1)}, bf16[1,192,1536]{2,1,0:T(8,128)(2,1)S(1)}, u32[]{:S(2)}, u32[]{:S(2)}) collective-permute-start(bf16[1,192,1536]{2,1,0:T(8,128)(2,1)S(1)} %get-tuple-element.20), channel_id=1, source_target_pairs={{0,4},{4,0},{8,12},{12,8},{16,20},{20,16},{24,28},{28,24},{1,5},{5... | collective-permute-start | bytes 1769480 | tf_op jit(solution)/shard_map/ppermute | solution.py:206
  113.3 3.7 %copy-done.1 = bf16[2,8,192,1536]{3,2,1,0:T(8,128)(2,1)S(1)} copy-done((bf16[2,8,192,1536]{3,2,1,0:T(8,128)(2,1)S(1)}, bf16[2,8,192,1536]{3,2,1,0:T(8,128)(2,1)}, u32[]{:S(2)}) %copy-start.1) | copy-done | bytes 9437208
  117.0 5.0 %shard_map.58 = (bf16[1,192,1536]{2,1,0:T(8,128)(2,1)}, f32[1,192,1536]{2,1,0:T(8,128)S(1)}) custom-call(s32[2]{0:T(128)S(1)} %get-tuple-element.23.where_ref, bf16[384,3072]{1,0:T(8,128)(2,1)S(1)} %bitcast.13, bf16[384,1536]{1,0:T(8,128)(2,1)S(1)} %copy-done.3, bf16[2,8,192,1536]{3,2,1,0:T(8,128)(2,1)S(1)} %copy-done.1), custom_call_target="tpu_custom_call" | custom-call | flops 905969664 | bytes 2359296 | tf_op jit(solution)/shard_map/pallas_call | solution.py:169
  122.0 5.5 %collective-permute-done.3 = bf16[1,192,1536]{2,1,0:T(8,128)(2,1)S(1)} collective-permute-done((bf16[1,192,1536]{2,1,0:T(8,128)(2,1)S(1)}, bf16[1,192,1536]{2,1,0:T(8,128)(2,1)S(1)}, u32[]{:S(2)}, u32[]{:S(2)}) %collective-permute-start.3) | collective-permute-done | bytes 589856 | tf_op jit(solution)/shard_map/ppermute | solution.py:206
  127.5 0.9 add_convert_fusion.2
  128.4 2.1 %collective-permute-start.4 = (bf16[1,192,1536]{2,1,0:T(8,128)(2,1)}, bf16[1,192,1536]{2,1,0:T(8,128)(2,1)}, u32[]{:S(2)}, u32[]{:S(2)}) collective-permute-start(bf16[1,192,1536]{2,1,0:T(8,128)(2,1)} %add_convert_fusion.2), channel_id=1, source_target_pairs={{0,8},{4,12},{8,16},{12,20},{16,24},{20,28},{24,0},{28,4},{1,9},{5... | collective-permute-start | bytes 1769480 | tf_op jit(solution)/shard_map/ppermute | solution.py:210
  130.6 0.1 pad_add_fusion
  130.6 3.7 %copy-done.2 = bf16[2,8,192,1536]{3,2,1,0:T(8,128)(2,1)S(1)} copy-done((bf16[2,8,192,1536]{3,2,1,0:T(8,128)(2,1)S(1)}, bf16[2,8,192,1536]{3,2,1,0:T(8,128)(2,1)}, u32[]{:S(2)}) %copy-start.2) | copy-done | bytes 9437208
  134.3 4.2 %shard_map.57 = (bf16[1,192,1536]{2,1,0:T(8,128)(2,1)S(1)}, f32[1,192,1536]{2,1,0:T(8,128)S(1)}) custom-call(s32[2]{0:T(128)S(1)} %get-tuple-element.22.where_ref, bf16[384,3072]{1,0:T(8,128)(2,1)S(1)} %bitcast.14, bf16[384,1536]{1,0:T(8,128)(2,1)S(1)} %copy-done.3, bf16[2,8,192,1536]{3,2,1,0:T(8,128)(2,1)S(1)} %copy-done.2), custom_call_target="tpu_custom_call" | custom-call | flops 905969664 | bytes 2359296 | tf_op jit(solution)/shard_map/pallas_call | solution.py:169
  138.5 1.6 collective-permute-start.1
  140.1 3.6 %collective-permute-done.4 = bf16[1,192,1536]{2,1,0:T(8,128)(2,1)} collective-permute-done((bf16[1,192,1536]{2,1,0:T(8,128)(2,1)}, bf16[1,192,1536]{2,1,0:T(8,128)(2,1)}, u32[]{:S(2)}, u32[]{:S(2)}) %collective-permute-start.4) | collective-permute-done | bytes 589856 | tf_op jit(solution)/shard_map/ppermute | solution.py:210
  143.6 1.4 add_convert_fusion.1
  145.1 4.2 %shard_map.56 = (bf16[1,192,1536]{2,1,0:T(8,128)(2,1)S(1)}, f32[1,192,1536]{2,1,0:T(8,128)S(1)}) custom-call(s32[2]{0:T(128)S(1)} %get-tuple-element.21.where_ref, bf16[384,3072]{1,0:T(8,128)(2,1)S(1)} %bitcast.15, bf16[384,1536]{1,0:T(8,128)(2,1)S(1)} %copy-done.3, bf16[2,8,192,1536]{3,2,1,0:T(8,128)(2,1)S(1)} %copy-done.2), custom_call_target="tpu_custom_call" | custom-call | flops 905969664 | bytes 2359296 | tf_op jit(solution)/shard_map/pallas_call | solution.py:169
  149.3 1.6 collective-permute-start
  150.9 3.7 %collective-permute-done.1 = bf16[1,192,1536]{2,1,0:T(8,128)(2,1)S(1)} collective-permute-done((bf16[1,192,1536]{2,1,0:T(8,128)(2,1)S(1)}, bf16[1,192,1536]{2,1,0:T(8,128)(2,1)S(1)}, u32[]{:S(2)}, u32[]{:S(2)}) %collective-permute-start.1) | collective-permute-done | bytes 589856 | tf_op jit(solution)/shard_map/ppermute | solution.py:206
  154.6 4.3 %collective-permute-done.5 = bf16[1,192,1536]{2,1,0:T(8,128)(2,1)S(1)} collective-permute-done((bf16[1,192,1536]{2,1,0:T(8,128)(2,1)S(1)}, bf16[1,192,1536]{2,1,0:T(8,128)(2,1)S(1)}, u32[]{:S(2)}, u32[]{:S(2)}) %collective-permute-start.5) | collective-permute-done | bytes 589856 | tf_op jit(solution)/shard_map/ppermute | solution.py:210
  158.8 0.2 add_convert_fusion
  159.1 5.1 %collective-permute-done = bf16[1,192,1536]{2,1,0:T(8,128)(2,1)S(1)} collective-permute-done((bf16[1,192,1536]{2,1,0:T(8,128)(2,1)S(1)}, bf16[1,192,1536]{2,1,0:T(8,128)(2,1)S(1)}, u32[]{:S(2)}, u32[]{:S(2)}) %collective-permute-start) | collective-permute-done | bytes 589856 | tf_op jit(solution)/shard_map/ppermute | solution.py:206
  164.3 7.7 %collective-permute-done.6 = bf16[1,192,1536]{2,1,0:T(8,128)(2,1)S(1)} collective-permute-done((bf16[1,192,1536]{2,1,0:T(8,128)(2,1)S(1)}, bf16[1,192,1536]{2,1,0:T(8,128)(2,1)S(1)}, u32[]{:S(2)}, u32[]{:S(2)}) %collective-permute-start.6) | collective-permute-done | bytes 589856 | tf_op jit(solution)/shard_map/ppermute | solution.py:210
  172.0 1.2 add_multiply_fusion
  (18 shorter events, 0.2 us)
Async XLA Ops:
  9.3 4.4 %copy-start.8 = (f32[48,128]{1,0:T(8,128)S(1)}, f32[48,128]{1,0:T(8,128)}, u32[]{:S(2)}) copy-start(f32[48,128]{1,0:T(8,128)} %param.8) | copy-start | bytes 73732
  9.3 32.9 %all-to-all-start = ((bf16[4,96,3072]{2,1,0:T(8,128)(2,1)}), bf16[4,96,3072]{2,1,0:T(8,128)(2,1)S(1)}, u32[]{:S(2)}, u32[]{:S(2)}) async-start(bf16[4,96,3072]{2,1,0:T(8,128)(2,1)} %bitcast.18), calls=%async_computation | async-start | bytes 4718592 | tf_op jit(solution)/shard_map/all_to_all | solution.py:228
  42.2 3.7 %copy-start.4 = (bf16[48,128,768]{2,1,0:T(8,128)(2,1)S(1)}, bf16[48,128,768]{2,1,0:T(8,128)(2,1)}, u32[]{:S(2)}) copy-start(bf16[48,128,768]{2,1,0:T(8,128)(2,1)} %legendre_ref.1) | copy-start | bytes 28311556
  69.5 1.4 copy-start.5
  70.9 32.2 %copy-start.3 = (bf16[384,1536]{1,0:T(8,128)(2,1)S(1)}, bf16[384,1536]{1,0:T(8,128)(2,1)}, u32[]{:S(2)}) copy-start(bf16[384,1536]{1,0:T(8,128)(2,1)} %constant.80.clone.table_ref) | copy-start | bytes 3538948
  70.9 32.2 %all-to-all-start.1 = ((bf16[4,96,3072]{2,1,0:T(8,128)(2,1)}), bf16[4,96,3072]{2,1,0:T(8,128)(2,1)S(1)}, u32[]{:S(2)}, u32[]{:S(2)}) async-start(bf16[4,96,3072]{2,1,0:T(8,128)(2,1)} %bitcast.16), calls=%async_computation.1 | async-start | bytes 4718592 | tf_op jit(solution)/shard_map/all_to_all | solution.py:232
  103.1 3.7 %copy-start = (bf16[2,8,192,1536]{3,2,1,0:T(8,128)(2,1)S(1)}, bf16[2,8,192,1536]{3,2,1,0:T(8,128)(2,1)}, u32[]{:S(2)}) copy-start(bf16[2,8,192,1536]{3,2,1,0:T(8,128)(2,1)} %weight_ref.7) | copy-start | bytes 28311556
  111.0 16.5 %collective-permute-start.3 = (bf16[1,192,1536]{2,1,0:T(8,128)(2,1)S(1)}, bf16[1,192,1536]{2,1,0:T(8,128)(2,1)S(1)}, u32[]{:S(2)}, u32[]{:S(2)}) collective-permute-start(bf16[1,192,1536]{2,1,0:T(8,128)(2,1)S(1)} %get-tuple-element.20), channel_id=1, source_target_pairs={{0,4},{4,0},{8,12},{12,8},{16,20},{20,16},{24,28},{28,24},{1,5},{5... | collective-permute-start | bytes 1769480 | tf_op jit(solution)/shard_map/ppermute | solution.py:206
  113.3 3.7 %copy-start.1 = (bf16[2,8,192,1536]{3,2,1,0:T(8,128)(2,1)S(1)}, bf16[2,8,192,1536]{3,2,1,0:T(8,128)(2,1)}, u32[]{:S(2)}) copy-start(bf16[2,8,192,1536]{3,2,1,0:T(8,128)(2,1)} %weight_ref.7) | copy-start | bytes 28311556
  122.0 6.4 %copy-start.6 = (f32[1,192,1536]{2,1,0:T(8,128)}, f32[1,192,1536]{2,1,0:T(8,128)S(1)}, u32[]{:S(2)}) copy-start(f32[1,192,1536]{2,1,0:T(8,128)S(1)} %get-tuple-element.17) | copy-start | bytes 3538948
  122.0 18.0 %collective-permute-start.2 = (bf16[1,192,1536]{2,1,0:T(8,128)(2,1)}, bf16[1,192,1536]{2,1,0:T(8,128)(2,1)}, u32[]{:S(2)}, u32[]{:S(2)}) collective-permute-start(bf16[1,192,1536]{2,1,0:T(8,128)(2,1)} %get-tuple-element.18), channel_id=1, source_target_pairs={{0,4},{4,0},{8,12},{12,8},{16,20},{20,16},{24,28},{28,24},{1,5},{5... | collective-permute-start | bytes 1769480 | tf_op jit(solution)/shard_map/ppermute | solution.py:206
  128.4 15.2 %collective-permute-start.4 = (bf16[1,192,1536]{2,1,0:T(8,128)(2,1)}, bf16[1,192,1536]{2,1,0:T(8,128)(2,1)}, u32[]{:S(2)}, u32[]{:S(2)}) collective-permute-start(bf16[1,192,1536]{2,1,0:T(8,128)(2,1)} %add_convert_fusion.2), channel_id=1, source_target_pairs={{0,8},{4,12},{8,16},{12,20},{16,24},{20,28},{24,0},{28,4},{1,9},{5... | collective-permute-start | bytes 1769480 | tf_op jit(solution)/shard_map/ppermute | solution.py:210
  130.6 3.7 %copy-start.2 = (bf16[2,8,192,1536]{3,2,1,0:T(8,128)(2,1)S(1)}, bf16[2,8,192,1536]{3,2,1,0:T(8,128)(2,1)}, u32[]{:S(2)}) copy-start(bf16[2,8,192,1536]{3,2,1,0:T(8,128)(2,1)} %weight_ref.7) | copy-start | bytes 28311556
  134.3 9.3 %copy-start.7 = (f32[1,192,1536]{2,1,0:T(8,128)S(1)}, f32[1,192,1536]{2,1,0:T(8,128)}, u32[]{:S(2)}) copy-start(f32[1,192,1536]{2,1,0:T(8,128)} %copy-done.6) | copy-start | bytes 3538948
  138.5 16.1 %collective-permute-start.1 = (bf16[1,192,1536]{2,1,0:T(8,128)(2,1)S(1)}, bf16[1,192,1536]{2,1,0:T(8,128)(2,1)S(1)}, u32[]{:S(2)}, u32[]{:S(2)}) collective-permute-start(bf16[1,192,1536]{2,1,0:T(8,128)(2,1)S(1)} %get-tuple-element.16), channel_id=1, source_target_pairs={{0,4},{4,0},{8,12},{12,8},{16,20},{20,16},{24,28},{28,24},{1,5},{5... | collective-permute-start | bytes 1769480 | tf_op jit(solution)/shard_map/ppermute | solution.py:206
  145.1 13.8 %collective-permute-start.5 = (bf16[1,192,1536]{2,1,0:T(8,128)(2,1)S(1)}, bf16[1,192,1536]{2,1,0:T(8,128)(2,1)S(1)}, u32[]{:S(2)}, u32[]{:S(2)}) collective-permute-start(bf16[1,192,1536]{2,1,0:T(8,128)(2,1)S(1)} %add_convert_fusion.1), channel_id=1, source_target_pairs={{0,8},{4,12},{8,16},{12,20},{16,24},{20,28},{24,0},{28,4},{1,9},{5... | collective-permute-start | bytes 1769480 | tf_op jit(solution)/shard_map/ppermute | solution.py:210
  149.3 14.9 %collective-permute-start = (bf16[1,192,1536]{2,1,0:T(8,128)(2,1)S(1)}, bf16[1,192,1536]{2,1,0:T(8,128)(2,1)S(1)}, u32[]{:S(2)}, u32[]{:S(2)}) collective-permute-start(bf16[1,192,1536]{2,1,0:T(8,128)(2,1)S(1)} %get-tuple-element.14), channel_id=1, source_target_pairs={{0,4},{4,0},{8,12},{12,8},{16,20},{20,16},{24,28},{28,24},{1,5},{5... | collective-permute-start | bytes 1769480 | tf_op jit(solution)/shard_map/ppermute | solution.py:206
  159.1 12.9 %collective-permute-start.6 = (bf16[1,192,1536]{2,1,0:T(8,128)(2,1)S(1)}, bf16[1,192,1536]{2,1,0:T(8,128)(2,1)S(1)}, u32[]{:S(2)}, u32[]{:S(2)}) collective-permute-start(bf16[1,192,1536]{2,1,0:T(8,128)(2,1)S(1)} %add_convert_fusion), channel_id=1, source_target_pairs={{0,8},{4,12},{8,16},{12,20},{16,24},{20,28},{24,0},{28,4},{1,9},{5... | collective-permute-start | bytes 1769480 | tf_op jit(solution)/shard_map/ppermute | solution.py:210

commit v2 on v1

--- a/solution.py
+++ b/solution.py
@@ -98,7 +98,7 @@
                 back_ref[src, part, pl.ds(wave, tiles, stride=waves), :] = block
         return carry
 
-    lax.fori_loop(0, waves, one_wave, 0)
+    lax.fori_loop(0, waves, one_wave, 0, unroll=4)
     for src in range(grid_count):
         for part in range(parts):
             for tile in range(tiles):
@@ -108,33 +108,118 @@
                 ].astype(jnp.bfloat16)
 
 
-def filter_packed(spectra, legendre, response, lat_dev, start, count):
-    grid_count, parts, _, points = spectra.shape
+def exchange_kernel(
+    lat_dev, spectra_ref, legendre_ref, response_ref, result_ref,
+    taken_ref, made_ref, basis_ref, rows_ref, back_ref,
+    basis_sem, own_sem, send_sem, recv_sem, done_sem, back_send_sem, back_recv_sem,
+):
+    chunks, grid_count, _, waves, _ = taken_ref.shape
+    me = lax.axis_index("grid")
+    peers = [lax.rem(me + d, grid_count) for d in range(1, grid_count)]
+
+    def basis_copy(c):
+        return pltpu.make_async_copy(legendre_ref.at[c], basis_ref.at[c], basis_sem.at[c])
+
+    def span(c):
+        return pl.ds(pl.multiple_of(c * waves, waves), waves)
+
+    def own_copy(c):
+        return pltpu.make_async_copy(
+            spectra_ref.at[me, :, span(c), :], taken_ref.at[c, me], own_sem.at[c]
+        )
+
+    def done_copy(c):
+        return pltpu.make_async_copy(
+            made_ref.at[c, me], result_ref.at[me, :, span(c), :], done_sem.at[c]
+        )
+
+    def out_copy(c, d):
+        return pltpu.make_async_remote_copy(
+            src_ref=spectra_ref.at[peers[d], :, span(c), :],
+            dst_ref=taken_ref.at[c, me],
+            send_sem=send_sem.at[c, d],
+            recv_sem=recv_sem.at[c, d],
+            device_id={"grid": peers[d]},
+            device_id_type=pl.DeviceIdType.MESH,
+        )
+
+    def back_copy(c, d):
+        return pltpu.make_async_remote_copy(
+            src_ref=made_ref.at[c, peers[d]],
+            dst_ref=result_ref.at[me, :, span(c), :],
+            send_sem=back_send_sem.at[c, d],
+            recv_sem=back_recv_sem.at[c, d],
+            device_id={"grid": peers[d]},
+            device_id_type=pl.DeviceIdType.MESH,
+        )
+
+    for c in range(chunks):
+        basis_copy(c).start()
+        own_copy(c).start()
+    barrier = pltpu.get_barrier_semaphore()
+    for peer in peers:
+        pl.semaphore_signal(
+            barrier, inc=1, device_id={"grid": peer}, device_id_type=pl.DeviceIdType.MESH
+        )
+    pl.semaphore_wait(barrier, grid_count - 1)
+    for c in range(chunks):
+        for d in range(grid_count - 1):
+            out_copy(c, d).start()
+
+    def one_chunk(c, carry):
+        basis_copy(c).wait()
+        own_copy(c).wait()
+        for d in range(grid_count - 1):
+            out_copy(c, d).wait_recv()
+        filter_kernel(
+            lat_dev, taken_ref.at[c], basis_ref.at[c], response_ref.at[c], made_ref.at[c], rows_ref, back_ref
+        )
+        done_copy(c).start()
+        for d in range(grid_count - 1):
+            back_copy(c, d).start()
+        return carry
+
+    lax.fori_loop(0, chunks, one_chunk, 0)
+    for c in range(chunks):
+        done_copy(c).wait()
+        for d in range(grid_count - 1):
+            out_copy(c, d).wait_send()
+            back_copy(c, d).wait()
+
+
+def filter_exchanged(spectra, legendre, response, lat_dev):
+    grid_count, parts, keep_dev, points = spectra.shape
     degrees, lat_count = legendre.shape[1:]
     waves = 16
-    first = start // waves
-    block = pl.BlockSpec((grid_count, parts, waves, points), lambda i: (0, 0, i, 0))
+    chunks = keep_dev // waves
+    stage = pltpu.VMEM((chunks, grid_count, parts, waves, points), jnp.bfloat16)
+    turned = pltpu.VMEM((grid_count, parts, points // 128 * waves, 128), jnp.float32)
+    one = pltpu.SemaphoreType.DMA((chunks,))
+    each = pltpu.SemaphoreType.DMA((chunks, grid_count - 1))
     return pl.pallas_call(
-        functools.partial(filter_kernel, lat_dev),
+        functools.partial(exchange_kernel, lat_dev),
         out_shape=jax.ShapeDtypeStruct(spectra.shape, jnp.bfloat16),
-        grid=(count // waves,),
         in_specs=[
-            block,
-            pl.BlockSpec((waves, degrees, lat_count), lambda i: (i + first, 0, 0)),
-            pl.BlockSpec((waves, degrees), lambda i: (i + first, 0)),
+            pl.BlockSpec(memory_space=pl.ANY),
+            pl.BlockSpec(memory_space=pl.ANY),
+            pl.BlockSpec(memory_space=pltpu.VMEM),
         ],
-        out_specs=block,
+        out_specs=pl.BlockSpec(memory_space=pl.ANY),
         scratch_shapes=[
-            pltpu.VMEM((grid_count, parts, points // 128 * waves, 128), jnp.float32),
-            pltpu.VMEM((grid_count, parts, points // 128 * waves, 128), jnp.float32),
+            stage, stage, pltpu.VMEM((chunks, waves, degrees, lat_count), jnp.bfloat16), turned, turned,
+            one, one, each, each, one, each, each,
         ],
-        compiler_params=pltpu.CompilerParams(vmem_limit_bytes=40 * 2**20),
+        compiler_params=pltpu.CompilerParams(
+            vmem_limit_bytes=56 * 2**20, collective_id=0, has_side_effects=True
+        ),
         cost_estimate=pl.CostEstimate(
-            flops=8 * count * degrees * lat_count * points // lat_dev,
-            bytes_accessed=2 * count * degrees * lat_count,
-            transcendentals=0,
-        ),
-    )(spectra, legendre, response)
+            flops=2**35, bytes_accessed=2 * keep_dev * degrees * lat_count, transcendentals=0
+        ),
+    )(
+        spectra,
+        legendre.reshape(chunks, waves, degrees, lat_count),
+        response.reshape(chunks, waves, degrees),
+    )
 
 
 def synth_kernel(where_ref, field_ref, table_ref, weight_ref, give_ref, keep_ref, total_ref):
@@ -183,7 +268,7 @@
             out_specs=(level, level),
             scratch_shapes=[pltpu.VMEM((2, lat_dev, wide), jnp.float32)],
         ),
-        compiler_params=pltpu.CompilerParams(vmem_limit_bytes=24 * 2**20),
+        compiler_params=pltpu.CompilerParams(vmem_limit_bytes=56 * 2**20),
         cost_estimate=pl.CostEstimate(
             flops=4 * mem_dev * lat_dev * cols * lon_count,
             bytes_accessed=4 * mem_dev * lat_dev * lon_count,
@@ -220,22 +305,9 @@
         table, alpha.reshape(points, lon_count), (((1,), (1,)), ((), ())), preferred_element_type=jnp.float32
     ).astype(jnp.bfloat16)
     spectra = spectra.reshape(grid_count, 2, keep_dev, points)
-    chunks = CHUNKS
-    step = keep_dev // chunks
-    pieces = []
-    for i in range(chunks):
-        piece = spectra[:, :, i * step : (i + 1) * step].reshape(grid_count, 2 * step, points)
-        piece = lax.all_to_all(piece, "grid", split_axis=0, concat_axis=0, tiled=True)
-        piece = piece.reshape(grid_count, 2, step, points)
-        piece = filter_packed(piece, legendre, response, lat_dev, i * step, step)
-        piece = piece.reshape(grid_count, 2 * step, points)
-        piece = lax.all_to_all(piece, "grid", split_axis=0, concat_axis=0, tiled=True)
-        pieces.append(piece.reshape(grid_count, 2, step, points))
-    filtered = jnp.concatenate(pieces, axis=2).reshape(grid_count * 2 * keep_dev, points)
+    filtered = filter_exchanged(spectra, legendre, response, lat_dev)
+    filtered = filtered.reshape(grid_count * 2 * keep_dev, points)
     return reduce_pairs(lambda goal, side: synth_pair(filtered, table, perturbation, goal, side))
-
-
-CHUNKS = 1
 
 
 def body(alpha, perturbation, legendre, response):

time: 174 us -> 141 us (0.81)
  waiting for transfers between devices: 86.6 us -> 34.5 us
  Pallas kernels: 41.1 us -> 86.1 us
  local copies, waits for them, and re-layouts: 16.2 us -> 0.02 us
  starting transfers between devices: 15.8 us -> 6.76 us
    all_to_all x2 -> x0, waiting for transfers between devices: 56.7 us -> none  [packed(): lax.all_to_all(piece, 'grid', split_axis=0, concat_axis=0, tiled=True)]
    pallas_call x1, Pallas kernels: 23.5 us -> 55.4 us  [filter_exchanged(): pl.pallas_call(functools.partial(exchange_kernel, lat_dev), out_shape=jax...]
    unnamed x18 -> x10, local copies, waits for them, and re-layouts: 16.2 us -> 0.02 us
    pallas_call x4, Pallas kernels: 17.6 us -> 30.7 us  [synth_pair(): pl.pallas_call(synth_kernel, out_shape=(jax.ShapeDtypeStruct((1, lat_dev,...]
    all_to_all x2 -> x0, starting transfers between devices: 8.15 us -> none  [packed(): lax.all_to_all(piece, 'grid', split_axis=0, concat_axis=0, tiled=True)]
    ppermute x3, waiting for transfers between devices: 15.6 us -> 21.1 us  [reduce_pairs(): total = lax.ppermute(here.astype(jnp.bfloat16), 'mem', onward)]
    convert_element_type x3, other arithmetic: 2.6 us -> 0.5 us  [reduce_pairs(): total = lax.ppermute(here.astype(jnp.bfloat16), 'mem', onward)]
  transfers between devices with their start and end apart: 9 -> 7, of which waited for: 8 -> 6; matrix products, arithmetic and copies ran while one was open for 2% -> 1% of each run, Pallas kernels for 8% -> 16%
where the time goes in v2:
time: 141 us
  Pallas kernels  86.1 us (61%)
  waiting for transfers between devices  34.5 us (24%)
  matrix products  9.32 us (7%)
  starting transfers between devices  6.76 us (5%)
  other arithmetic  3.73 us (3%)
    pallas_call x1, Pallas kernels, filter_exchanged(): pl.pallas_call(functools.partial(exchange_kernel, lat_dev), out_shape=jax...  55.4 us
    pallas_call x4, Pallas kernels, synth_pair(): pl.pallas_call(synth_kernel, out_shape=(jax.ShapeDtypeStruct((1, lat_dev,...  30.7 us
    ppermute x3, waiting for transfers between devices, reduce_pairs(): total = lax.ppermute(here.astype(jnp.bfloat16), 'mem', onward)  21.1 us
    ppermute x4, waiting for transfers between devices, reduce_pairs(): here = here + lax.ppermute(give, 'mem', swap).astype(jnp.float32)  13.4 us
    dot_general x1, matrix products, packed(): lax.dot_general(table, alpha.reshape(points, lon_count), (((1,), (1,)), (...  9.32 us
    ppermute x4, starting transfers between devices, reduce_pairs(): here = here + lax.ppermute(give, 'mem', swap).astype(jnp.float32)  5.02 us
  transfers between devices with their start and end apart: 7, of which 6 were waited for; matrix products, arithmetic and copies ran while one was open for 1% of the time, Pallas kernels for 16%

profile of v2, /device:TPU:0, one launch (start us, length us, event | category | flops | bytes accessed | tf_op | source)
XLA Modules:
  0.0 140.5 jit_solution(2130646692265597446)
XLA Ops:
  0.0 9.3 %convolution_convert_fusion = bf16[384,3072]{1,0:T(8,128)(2,1)} fusion(bf16[384,1536]{1,0:T(8,128)(2,1)} %constant.80.clone.table_ref, bf16[3072,1536]{1,0:T(8,128)(2,1)} %bitcast.17), kind=kOutput, calls=%fused_computation | convolution fusion | flops 3625058304 | bytes 12976128 | tf_op jit(solution)/shard_map/dot_general | solution.py:304
  9.3 0.0 copy-done.4
  9.3 0.7 broadcast_multiply_fusion
  10.0 0.7 pad_add_fusion.2
  10.7 55.4 %shard_map.55 = bf16[4,2,48,3072]{3,2,1,0:T(8,128)(2,1)} custom-call(bf16[4,2,48,3072]{3,2,1,0:T(8,128)(2,1)} %bitcast.19, bf16[3,16,128,768]{3,2,1,0:T(8,128)(2,1)} %bitcast.18, f32[3,16,128]{2,1,0:T(8,128)} %bitcast.16), custom_call_target="tpu_custom_call" | custom-call | flops 34359738368 | bytes 9437184 | tf_op jit(solution)/shard_map/pallas_call | solution.py:199
  66.1 7.6 %shard_map.59 = (bf16[1,192,1536]{2,1,0:T(8,128)(2,1)}, f32[1,192,1536]{2,1,0:T(8,128)}) custom-call(s32[2]{0:T(128)} %get-tuple-element.24.where_ref, bf16[384,3072]{1,0:T(8,128)(2,1)} %bitcast.12, bf16[384,1536]{1,0:T(8,128)(2,1)} %constant.80.clone.table_ref, bf16[2,8,192,1536]{3,2,1,0:T(8,128)(2,1)} %weight_ref.7), custom_call_target="tpu_custom_call" | custom-call | flops 905969664 | bytes 2359296 | tf_op jit(solution)/shard_map/pallas_call | solution.py:254
  73.7 1.5 %collective-permute-start.3 = (bf16[1,192,1536]{2,1,0:T(8,128)(2,1)}, bf16[1,192,1536]{2,1,0:T(8,128)(2,1)S(1)}, u32[]{:S(2)}, u32[]{:S(2)}) collective-permute-start(bf16[1,192,1536]{2,1,0:T(8,128)(2,1)} %get-tuple-element.20), channel_id=1, source_target_pairs={{0,4},{4,0},{8,12},{12,8},{16,20},{20,16},{24,28},{28,24},{1,5},{5... | collective-permute-start | bytes 1769480 | tf_op jit(solution)/shard_map/ppermute | solution.py:291
  75.2 7.7 %shard_map.58 = (bf16[1,192,1536]{2,1,0:T(8,128)(2,1)}, f32[1,192,1536]{2,1,0:T(8,128)}) custom-call(s32[2]{0:T(128)} %get-tuple-element.23.where_ref, bf16[384,3072]{1,0:T(8,128)(2,1)} %bitcast.13, bf16[384,1536]{1,0:T(8,128)(2,1)} %constant.80.clone.table_ref, bf16[2,8,192,1536]{3,2,1,0:T(8,128)(2,1)} %weight_ref.7), custom_call_target="tpu_custom_call" | custom-call | flops 905969664 | bytes 2359296 | tf_op jit(solution)/shard_map/pallas_call | solution.py:254
  82.9 0.5 collective-permute-start.2
  83.4 6.6 %collective-permute-done.3 = bf16[1,192,1536]{2,1,0:T(8,128)(2,1)S(1)} collective-permute-done((bf16[1,192,1536]{2,1,0:T(8,128)(2,1)}, bf16[1,192,1536]{2,1,0:T(8,128)(2,1)S(1)}, u32[]{:S(2)}, u32[]{:S(2)}) %collective-permute-start.3) | collective-permute-done | bytes 589856 | tf_op jit(solution)/shard_map/ppermute | solution.py:291
  90.1 0.0 copy-done.1
  90.1 0.1 add_convert_fusion.2
  90.2 1.6 %collective-permute-start.4 = (bf16[1,192,1536]{2,1,0:T(8,128)(2,1)S(1)}, bf16[1,192,1536]{2,1,0:T(8,128)(2,1)S(1)}, u32[]{:S(2)}, u32[]{:S(2)}) collective-permute-start(bf16[1,192,1536]{2,1,0:T(8,128)(2,1)S(1)} %add_convert_fusion.2), channel_id=1, source_target_pairs={{0,8},{4,12},{8,16},{12,20},{16,24},{20,28},{24,0},{28,4},{1,9},{5... | collective-permute-start | bytes 1769480 | tf_op jit(solution)/shard_map/ppermute | solution.py:295
  91.8 0.7 pad_add_fusion
  92.5 7.7 %shard_map.57 = (bf16[1,192,1536]{2,1,0:T(8,128)(2,1)}, f32[1,192,1536]{2,1,0:T(8,128)}) custom-call(s32[2]{0:T(128)} %get-tuple-element.22.where_ref, bf16[384,3072]{1,0:T(8,128)(2,1)} %bitcast.14, bf16[384,1536]{1,0:T(8,128)(2,1)} %constant.80.clone.table_ref, bf16[2,8,192,1536]{3,2,1,0:T(8,128)(2,1)} %weight_ref.7), custom_call_target="tpu_custom_call" | custom-call | flops 905969664 | bytes 2359296 | tf_op jit(solution)/shard_map/pallas_call | solution.py:254
  100.2 1.5 %collective-permute-start.1 = (bf16[1,192,1536]{2,1,0:T(8,128)(2,1)}, bf16[1,192,1536]{2,1,0:T(8,128)(2,1)S(1)}, u32[]{:S(2)}, u32[]{:S(2)}) collective-permute-start(bf16[1,192,1536]{2,1,0:T(8,128)(2,1)} %get-tuple-element.16), channel_id=1, source_target_pairs={{0,4},{4,0},{8,12},{12,8},{16,20},{20,16},{24,28},{28,24},{1,5},{5... | collective-permute-start | bytes 1769480 | tf_op jit(solution)/shard_map/ppermute | solution.py:291
  101.7 0.8 collective-permute-done.2
  102.5 4.8 %collective-permute-done.4 = bf16[1,192,1536]{2,1,0:T(8,128)(2,1)S(1)} collective-permute-done((bf16[1,192,1536]{2,1,0:T(8,128)(2,1)S(1)}, bf16[1,192,1536]{2,1,0:T(8,128)(2,1)S(1)}, u32[]{:S(2)}, u32[]{:S(2)}) %collective-permute-start.4) | collective-permute-done | bytes 589856 | tf_op jit(solution)/shard_map/ppermute | solution.py:295
  107.3 0.0 copy-done.2
  107.3 0.2 add_convert_fusion.1
  107.5 0.1 collective-permute-start.5
  107.6 0.0 copy-start.3
  107.6 7.7 %shard_map.56 = (bf16[1,192,1536]{2,1,0:T(8,128)(2,1)}, f32[1,192,1536]{2,1,0:T(8,128)}) custom-call(s32[2]{0:T(128)} %get-tuple-element.21.where_ref, bf16[384,3072]{1,0:T(8,128)(2,1)} %bitcast.15, bf16[384,1536]{1,0:T(8,128)(2,1)} %constant.80.clone.table_ref, bf16[2,8,192,1536]{3,2,1,0:T(8,128)(2,1)} %weight_ref.7), custom_call_target="tpu_custom_call" | custom-call | flops 905969664 | bytes 2359296 | tf_op jit(solution)/shard_map/pallas_call | solution.py:254
  115.3 1.5 %collective-permute-start = (bf16[1,192,1536]{2,1,0:T(8,128)(2,1)}, bf16[1,192,1536]{2,1,0:T(8,128)(2,1)S(1)}, u32[]{:S(2)}, u32[]{:S(2)}) collective-permute-start(bf16[1,192,1536]{2,1,0:T(8,128)(2,1)} %get-tuple-element.14), channel_id=1, source_target_pairs={{0,4},{4,0},{8,12},{12,8},{16,20},{20,16},{24,28},{28,24},{1,5},{5... | collective-permute-start | bytes 1769480 | tf_op jit(solution)/shard_map/ppermute | solution.py:291
  116.8 0.0 collective-permute-done.1
  116.8 6.9 %collective-permute-done.5 = bf16[1,192,1536]{2,1,0:T(8,128)(2,1)S(1)} collective-permute-done((bf16[1,192,1536]{2,1,0:T(8,128)(2,1)S(1)}, bf16[1,192,1536]{2,1,0:T(8,128)(2,1)S(1)}, u32[]{:S(2)}, u32[]{:S(2)}) %collective-permute-start.5) | collective-permute-done | bytes 589856 | tf_op jit(solution)/shard_map/ppermute | solution.py:295
  123.7 0.2 add_convert_fusion
  123.9 0.1 collective-permute-start.6
  124.0 5.9 %collective-permute-done = bf16[1,192,1536]{2,1,0:T(8,128)(2,1)S(1)} collective-permute-done((bf16[1,192,1536]{2,1,0:T(8,128)(2,1)}, bf16[1,192,1536]{2,1,0:T(8,128)(2,1)S(1)}, u32[]{:S(2)}, u32[]{:S(2)}) %collective-permute-start) | collective-permute-done | bytes 589856 | tf_op jit(solution)/shard_map/ppermute | solution.py:291
  129.9 9.4 %collective-permute-done.6 = bf16[1,192,1536]{2,1,0:T(8,128)(2,1)S(1)} collective-permute-done((bf16[1,192,1536]{2,1,0:T(8,128)(2,1)S(1)}, bf16[1,192,1536]{2,1,0:T(8,128)(2,1)S(1)}, u32[]{:S(2)}, u32[]{:S(2)}) %collective-permute-start.6) | collective-permute-done | bytes 589856 | tf_op jit(solution)/shard_map/ppermute | solution.py:295
  139.3 0.0 copy-done
  139.3 1.2 add_multiply_fusion
  (6 shorter events, 0.0 us)
Async XLA Ops:
  0.0 9.3 %copy-start.4 = (f32[48,128]{1,0:T(8,128)S(1)}, f32[48,128]{1,0:T(8,128)}, u32[]{:S(2)}) copy-start(f32[48,128]{1,0:T(8,128)} %param.8) | copy-start | bytes 73732
  73.7 16.4 %collective-permute-start.3 = (bf16[1,192,1536]{2,1,0:T(8,128)(2,1)}, bf16[1,192,1536]{2,1,0:T(8,128)(2,1)S(1)}, u32[]{:S(2)}, u32[]{:S(2)}) collective-permute-start(bf16[1,192,1536]{2,1,0:T(8,128)(2,1)} %get-tuple-element.20), channel_id=1, source_target_pairs={{0,4},{4,0},{8,12},{12,8},{16,20},{20,16},{24,28},{28,24},{1,5},{5... | collective-permute-start | bytes 1769480 | tf_op jit(solution)/shard_map/ppermute | solution.py:291
  75.2 14.9 %copy-start.1 = (f32[1,192,1536]{2,1,0:T(8,128)S(1)}, f32[1,192,1536]{2,1,0:T(8,128)}, u32[]{:S(2)}) copy-start(f32[1,192,1536]{2,1,0:T(8,128)} %get-tuple-element.19) | copy-start | bytes 3538948
  82.9 19.6 %collective-permute-start.2 = (bf16[1,192,1536]{2,1,0:T(8,128)(2,1)}, bf16[1,192,1536]{2,1,0:T(8,128)(2,1)S(1)}, u32[]{:S(2)}, u32[]{:S(2)}) collective-permute-start(bf16[1,192,1536]{2,1,0:T(8,128)(2,1)} %get-tuple-element.18), channel_id=1, source_target_pairs={{0,4},{4,0},{8,12},{12,8},{16,20},{20,16},{24,28},{28,24},{1,5},{5... | collective-permute-start | bytes 1769480 | tf_op jit(solution)/shard_map/ppermute | solution.py:291
  90.2 17.1 %collective-permute-start.4 = (bf16[1,192,1536]{2,1,0:T(8,128)(2,1)S(1)}, bf16[1,192,1536]{2,1,0:T(8,128)(2,1)S(1)}, u32[]{:S(2)}, u32[]{:S(2)}) collective-permute-start(bf16[1,192,1536]{2,1,0:T(8,128)(2,1)S(1)} %add_convert_fusion.2), channel_id=1, source_target_pairs={{0,8},{4,12},{8,16},{12,20},{16,24},{20,28},{24,0},{28,4},{1,9},{5... | collective-permute-start | bytes 1769480 | tf_op jit(solution)/shard_map/ppermute | solution.py:295
  92.5 14.8 %copy-start.2 = (f32[1,192,1536]{2,1,0:T(8,128)S(1)}, f32[1,192,1536]{2,1,0:T(8,128)}, u32[]{:S(2)}) copy-start(f32[1,192,1536]{2,1,0:T(8,128)} %get-tuple-element.17) | copy-start | bytes 3538948
  100.2 16.6 %collective-permute-start.1 = (bf16[1,192,1536]{2,1,0:T(8,128)(2,1)}, bf16[1,192,1536]{2,1,0:T(8,128)(2,1)S(1)}, u32[]{:S(2)}, u32[]{:S(2)}) collective-permute-start(bf16[1,192,1536]{2,1,0:T(8,128)(2,1)} %get-tuple-element.16), channel_id=1, source_target_pairs={{0,4},{4,0},{8,12},{12,8},{16,20},{20,16},{24,28},{28,24},{1,5},{5... | collective-permute-start | bytes 1769480 | tf_op jit(solution)/shard_map/ppermute | solution.py:291
  107.5 16.2 %collective-permute-start.5 = (bf16[1,192,1536]{2,1,0:T(8,128)(2,1)S(1)}, bf16[1,192,1536]{2,1,0:T(8,128)(2,1)S(1)}, u32[]{:S(2)}, u32[]{:S(2)}) collective-permute-start(bf16[1,192,1536]{2,1,0:T(8,128)(2,1)S(1)} %add_convert_fusion.1), channel_id=1, source_target_pairs={{0,8},{4,12},{8,16},{12,20},{16,24},{20,28},{24,0},{28,4},{1,9},{5... | collective-permute-start | bytes 1769480 | tf_op jit(solution)/shard_map/ppermute | solution.py:295
  107.6 16.2 %copy-start.3 = (f32[1,192,1536]{2,1,0:T(8,128)S(1)}, f32[1,192,1536]{2,1,0:T(8,128)}, u32[]{:S(2)}) copy-start(f32[1,192,1536]{2,1,0:T(8,128)} %get-tuple-element.15) | copy-start | bytes 3538948
  115.3 14.6 %collective-permute-start = (bf16[1,192,1536]{2,1,0:T(8,128)(2,1)}, bf16[1,192,1536]{2,1,0:T(8,128)(2,1)S(1)}, u32[]{:S(2)}, u32[]{:S(2)}) collective-permute-start(bf16[1,192,1536]{2,1,0:T(8,128)(2,1)} %get-tuple-element.14), channel_id=1, source_target_pairs={{0,4},{4,0},{8,12},{12,8},{16,20},{20,16},{24,28},{28,24},{1,5},{5... | collective-permute-start | bytes 1769480 | tf_op jit(solution)/shard_map/ppermute | solution.py:291
  123.7 15.6 %copy-start = (f32[1,192,1536]{2,1,0:T(8,128)S(1)}, f32[1,192,1536]{2,1,0:T(8,128)}, u32[]{:S(2)}) copy-start(f32[1,192,1536]{2,1,0:T(8,128)} %get-tuple-element.13) | copy-start | bytes 3538948
  123.9 15.4 %collective-permute-start.6 = (bf16[1,192,1536]{2,1,0:T(8,128)(2,1)S(1)}, bf16[1,192,1536]{2,1,0:T(8,128)(2,1)S(1)}, u32[]{:S(2)}, u32[]{:S(2)}) collective-permute-start(bf16[1,192,1536]{2,1,0:T(8,128)(2,1)S(1)} %add_convert_fusion), channel_id=1, source_target_pairs={{0,8},{4,12},{8,16},{12,20},{16,24},{20,28},{24,0},{28,4},{1,9},{5... | collective-permute-start | bytes 1769480 | tf_op jit(solution)/shard_map/ppermute | solution.py:295

commit v3 on v2

--- a/solution.py
+++ b/solution.py
@@ -245,55 +245,59 @@
         keep_ref[0] = total_ref[side]
 
 
-def synth_pair(filtered, table, perturbation, goal, side):
+def synth_pair(filtered, table, perturbation, goal, side, strip, strips):
     mem_dev, levels, lat_dev, lon_count = perturbation.shape
     cols = table.shape[0]
     pairs = levels // 2
-    wide = math.gcd(lon_count, 512)
+    strip_lon = lon_count // strips
+    wide = strip_lon
+    first = strip * (strip_lon // wide)
     level = pl.BlockSpec((1, lat_dev, wide), lambda i, k, w: (0, 0, i))
     return pl.pallas_call(
         synth_kernel,
         out_shape=(
-            jax.ShapeDtypeStruct((1, lat_dev, lon_count), jnp.bfloat16),
-            jax.ShapeDtypeStruct((1, lat_dev, lon_count), jnp.float32),
+            jax.ShapeDtypeStruct((1, lat_dev, strip_lon), jnp.bfloat16),
+            jax.ShapeDtypeStruct((1, lat_dev, strip_lon), jnp.float32),
         ),
         grid_spec=pltpu.PrefetchScalarGridSpec(
             num_scalar_prefetch=1,
-            grid=(lon_count // wide, mem_dev),
+            grid=(strip_lon // wide, mem_dev),
             in_specs=[
                 pl.BlockSpec((cols, 2 * lat_dev), lambda i, k, w: (0, k * pairs + w[0])),
-                pl.BlockSpec((cols, wide), lambda i, k, w: (0, i)),
-                pl.BlockSpec((1, 2, lat_dev, wide), lambda i, k, w: (k, w[0], 0, i)),
+                pl.BlockSpec((cols, wide), lambda i, k, w: (0, i + first)),
+                pl.BlockSpec((1, 2, lat_dev, wide), lambda i, k, w: (k, w[0], 0, i + first)),
             ],
             out_specs=(level, level),
             scratch_shapes=[pltpu.VMEM((2, lat_dev, wide), jnp.float32)],
         ),
         compiler_params=pltpu.CompilerParams(vmem_limit_bytes=56 * 2**20),
         cost_estimate=pl.CostEstimate(
-            flops=4 * mem_dev * lat_dev * cols * lon_count,
-            bytes_accessed=4 * mem_dev * lat_dev * lon_count,
+            flops=4 * mem_dev * lat_dev * cols * strip_lon,
+            bytes_accessed=4 * mem_dev * lat_dev * strip_lon,
             transcendentals=0,
         ),
     )(jnp.stack([goal, side]).astype(jnp.int32), filtered, table, perturbation)
 
 
-def reduce_pairs(both):
+def reduce_pairs(both, strips):
     mem_count = lax.axis_size("mem")
     me = lax.axis_index("mem")
     ring = mem_count // 2
     side, place = me % 2, me // 2
     swap = [(j, j ^ 1) for j in range(mem_count)]
     onward = [(j, (j + 2) % mem_count) for j in range(mem_count)]
-    total = None
+    totals = [None] * strips
     for step in range(ring):
         goal = (place + 2 * ring - 1 - step) % ring
-        give, here = both(goal, side)
-        here = here + lax.ppermute(give, "mem", swap).astype(jnp.float32)
-        if total is not None:
-            here = here + total.astype(jnp.float32)
-        if step < ring - 1:
-            total = lax.ppermute(here.astype(jnp.bfloat16), "mem", onward)
-    return here
+        for strip in range(strips):
+            give, here = both(goal, side, strip)
+            here = here + lax.ppermute(give, "mem", swap).astype(jnp.float32)
+            if step > 0:
+                here = here + totals[strip].astype(jnp.float32)
+            if step < ring - 1:
+                here = lax.ppermute(here.astype(jnp.bfloat16), "mem", onward)
+            totals[strip] = here
+    return jnp.concatenate(totals, axis=2)
 
 
 def packed(alpha, perturbation, legendre, response, table):
@@ -307,7 +311,12 @@
     spectra = spectra.reshape(grid_count, 2, keep_dev, points)
     filtered = filter_exchanged(spectra, legendre, response, lat_dev)
     filtered = filtered.reshape(grid_count * 2 * keep_dev, points)
-    return reduce_pairs(lambda goal, side: synth_pair(filtered, table, perturbation, goal, side))
+    strips = 2 if lon_count % 256 == 0 else 1
+
+    def both(goal, side, strip):
+        return synth_pair(filtered, table, perturbation, goal, side, strip, strips)
+
+    return reduce_pairs(both, strips)
 
 
 def body(alpha, perturbation, legendre, response):

time: 141 us -> 138 us (0.979)
  waiting for transfers between devices: 34.5 us -> 21.3 us
  starting transfers between devices: 6.76 us -> 12.5 us
  Pallas kernels: 86.1 us -> 89.8 us
    ppermute x4 -> x8, waiting for transfers between devices: 13.4 us -> 0.02 us  [reduce_pairs(): here = here + lax.ppermute(give, 'mem', swap).astype(jnp.float32)]
    pallas_call x4 -> x8, Pallas kernels: 30.7 us -> 34.4 us  [synth_pair(): pl.pallas_call(synth_kernel, out_shape=(jax.ShapeDtypeStruct((1, lat_dev,...]
    ppermute x4 -> x8, starting transfers between devices: 5.02 us -> 8.03 us  [reduce_pairs(): here = here + lax.ppermute(give, 'mem', swap).astype(jnp.float32)]
    ppermute x3 -> x6, starting transfers between devices: 1.74 us -> 4.46 us  [reduce_pairs(): here = lax.ppermute(here.astype(jnp.bfloat16), 'mem', onward)]
    ppermute x3 -> x6, waiting for transfers between devices: 21.1 us -> 21.3 us  [reduce_pairs(): here = lax.ppermute(here.astype(jnp.bfloat16), 'mem', onward)]
  transfers between devices with their start and end apart: 7 -> 14, of which waited for: 6 -> 6; matrix products, arithmetic and copies ran while one was open for 1% -> 1% of each run, Pallas kernels for 16% -> 22%
where the time goes in v3:
time: 138 us
  Pallas kernels  89.8 us (65%)
  waiting for transfers between devices  21.3 us (15%)
  starting transfers between devices  12.5 us (9%)
  matrix products  9.35 us (7%)
  other arithmetic  4.47 us (3%)
    pallas_call x1, Pallas kernels, filter_exchanged(): pl.pallas_call(functools.partial(exchange_kernel, lat_dev), out_shape=jax...  55.4 us
    pallas_call x8, Pallas kernels, synth_pair(): pl.pallas_call(synth_kernel, out_shape=(jax.ShapeDtypeStruct((1, lat_dev,...  34.4 us
    ppermute x6, waiting for transfers between devices, reduce_pairs(): here = lax.ppermute(here.astype(jnp.bfloat16), 'mem', onward)  21.3 us
    dot_general x1, matrix products, packed(): lax.dot_general(table, alpha.reshape(points, lon_count), (((1,), (1,)), (...  9.35 us
    ppermute x8, starting transfers between devices, reduce_pairs(): here = here + lax.ppermute(give, 'mem', swap).astype(jnp.float32)  8.03 us
    ppermute x6, starting transfers between devices, reduce_pairs(): here = lax.ppermute(here.astype(jnp.bfloat16), 'mem', onward)  4.46 us
  transfers between devices with their start and end apart: 14, of which 6 were waited for; matrix products, arithmetic and copies ran while one was open for 1% of the time, Pallas kernels for 22%

profile of v3, /device:TPU:0, one launch (start us, length us, event | category | flops | bytes accessed | tf_op | source)
XLA Modules:
  0.0 137.6 jit_solution(10986242600484354565)
XLA Ops:
  0.0 1.4 %broadcast_multiply_fusion = f32[48,128]{1,0:T(8,128)} fusion(f32[48,128]{1,0:T(8,128)} %param.8, f32[48]{0:T(128)S(1)} %compare_select_fusion), kind=kLoop, calls=%fused_computation.10 | loop fusion | flops 6144 | bytes 49344 | tf_op jit(solution)/shard_map/mul | solution.py:330
  1.4 9.3 %convolution_convert_fusion = bf16[384,3072]{1,0:T(8,128)(2,1)} fusion(bf16[384,1536]{1,0:T(8,128)(2,1)} %constant.80.clone.table_ref, bf16[3072,1536]{1,0:T(8,128)(2,1)} %bitcast.21), kind=kOutput, calls=%fused_computation | convolution fusion | flops 3625058304 | bytes 12976128 | tf_op jit(solution)/shard_map/dot_general | solution.py:308
  10.8 0.7 pad_add_fusion.2
  11.4 55.4 %shard_map.55 = bf16[4,2,48,3072]{3,2,1,0:T(8,128)(2,1)} custom-call(bf16[4,2,48,3072]{3,2,1,0:T(8,128)(2,1)} %bitcast.23, bf16[3,16,128,768]{3,2,1,0:T(8,128)(2,1)} %bitcast.22, f32[3,16,128]{2,1,0:T(8,128)} %bitcast.20), custom_call_target="tpu_custom_call" | custom-call | flops 34359738368 | bytes 9437184 | tf_op jit(solution)/shard_map/pallas_call | solution.py:199
  66.9 4.2 %shard_map.63 = (bf16[1,192,768]{2,1,0:T(8,128)(2,1)}, f32[1,192,768]{2,1,0:T(8,128)}) custom-call(s32[2]{0:T(128)} %get-tuple-element.40.where_ref, bf16[384,3072]{1,0:T(8,128)(2,1)} %bitcast.12, bf16[384,1536]{1,0:T(8,128)(2,1)} %constant.80.clone.table_ref, bf16[2,8,192,1536]{3,2,1,0:T(8,128)(2,1)} %weight_ref.15), custom_call_target="tpu_custom_call" | custom-call | flops 452984832 | bytes 1179648 | tf_op jit(solution)/shard_map/pallas_call | solution.py:256
  71.1 1.5 %collective-permute-start.10 = (bf16[1,192,768]{2,1,0:T(8,128)(2,1)}, bf16[1,192,768]{2,1,0:T(8,128)(2,1)S(1)}, u32[]{:S(2)}, u32[]{:S(2)}) collective-permute-start(bf16[1,192,768]{2,1,0:T(8,128)(2,1)} %get-tuple-element.36), channel_id=1, source_target_pairs={{0,4},{4,0},{8,12},{12,8},{16,20},{20,16},{24,28},{28,24},{1,5},{5... | collective-permute-start | bytes 884744 | tf_op jit(solution)/shard_map/ppermute | solution.py:294
  72.6 4.2 %shard_map.59 = (bf16[1,192,768]{2,1,0:T(8,128)(2,1)}, f32[1,192,768]{2,1,0:T(8,128)}) custom-call(s32[2]{0:T(128)} %get-tuple-element.40.where_ref, bf16[384,3072]{1,0:T(8,128)(2,1)} %bitcast.13, bf16[384,1536]{1,0:T(8,128)(2,1)} %constant.80.clone.table_ref, bf16[2,8,192,1536]{3,2,1,0:T(8,128)(2,1)} %weight_ref.15), custom_call_target="tpu_custom_call" | custom-call | flops 452984832 | bytes 1179648 | tf_op jit(solution)/shard_map/pallas_call | solution.py:256
  76.8 0.5 collective-permute-start.3
  77.4 4.2 %shard_map.62 = (bf16[1,192,768]{2,1,0:T(8,128)(2,1)}, f32[1,192,768]{2,1,0:T(8,128)}) custom-call(s32[2]{0:T(128)} %get-tuple-element.39.where_ref, bf16[384,3072]{1,0:T(8,128)(2,1)} %bitcast.14, bf16[384,1536]{1,0:T(8,128)(2,1)} %constant.80.clone.table_ref, bf16[2,8,192,1536]{3,2,1,0:T(8,128)(2,1)} %weight_ref.15), custom_call_target="tpu_custom_call" | custom-call | flops 452984832 | bytes 1179648 | tf_op jit(solution)/shard_map/pallas_call | solution.py:256
  81.6 1.5 %collective-permute-start.9 = (bf16[1,192,768]{2,1,0:T(8,128)(2,1)}, bf16[1,192,768]{2,1,0:T(8,128)(2,1)S(1)}, u32[]{:S(2)}, u32[]{:S(2)}) collective-permute-start(bf16[1,192,768]{2,1,0:T(8,128)(2,1)} %get-tuple-element.34), channel_id=1, source_target_pairs={{0,4},{4,0},{8,12},{12,8},{16,20},{20,16},{24,28},{28,24},{1,5},{5... | collective-permute-start | bytes 884744 | tf_op jit(solution)/shard_map/ppermute | solution.py:294
  83.1 4.3 %shard_map.58 = (bf16[1,192,768]{2,1,0:T(8,128)(2,1)}, f32[1,192,768]{2,1,0:T(8,128)}) custom-call(s32[2]{0:T(128)} %get-tuple-element.39.where_ref, bf16[384,3072]{1,0:T(8,128)(2,1)} %bitcast.15, bf16[384,1536]{1,0:T(8,128)(2,1)} %constant.80.clone.table_ref, bf16[2,8,192,1536]{3,2,1,0:T(8,128)(2,1)} %weight_ref.15), custom_call_target="tpu_custom_call" | custom-call | flops 452984832 | bytes 1179648 | tf_op jit(solution)/shard_map/pallas_call | solution.py:256
  87.3 0.5 collective-permute-start.2
  87.9 0.6 pad_add_fusion
  88.5 4.4 %shard_map.61 = (bf16[1,192,768]{2,1,0:T(8,128)(2,1)}, f32[1,192,768]{2,1,0:T(8,128)}) custom-call(s32[2]{0:T(128)} %get-tuple-element.38.where_ref, bf16[384,3072]{1,0:T(8,128)(2,1)} %bitcast.16, bf16[384,1536]{1,0:T(8,128)(2,1)} %constant.80.clone.table_ref, bf16[2,8,192,1536]{3,2,1,0:T(8,128)(2,1)} %weight_ref.15), custom_call_target="tpu_custom_call" | custom-call | flops 452984832 | bytes 1179648 | tf_op jit(solution)/shard_map/pallas_call | solution.py:256
  92.8 1.5 %collective-permute-start.8 = (bf16[1,192,768]{2,1,0:T(8,128)(2,1)}, bf16[1,192,768]{2,1,0:T(8,128)(2,1)S(1)}, u32[]{:S(2)}, u32[]{:S(2)}) collective-permute-start(bf16[1,192,768]{2,1,0:T(8,128)(2,1)} %get-tuple-element.32), channel_id=1, source_target_pairs={{0,4},{4,0},{8,12},{12,8},{16,20},{20,16},{24,28},{28,24},{1,5},{5... | collective-permute-start | bytes 884744 | tf_op jit(solution)/shard_map/ppermute | solution.py:294
  94.4 1.6 %collective-permute-start.11 = (bf16[1,192,768]{2,1,0:T(8,128)(2,1)S(1)}, bf16[1,192,768]{2,1,0:T(8,128)(2,1)S(1)}, u32[]{:S(2)}, u32[]{:S(2)}) collective-permute-start(bf16[1,192,768]{2,1,0:T(8,128)(2,1)S(1)} %add_convert_fusion.2), channel_id=1, source_target_pairs={{0,8},{4,12},{8,16},{12,20},{16,24},{20,28},{24,0},{28,4},{1,9},{5... | collective-permute-start | bytes 884744 | tf_op jit(solution)/shard_map/ppermute | solution.py:298
  96.0 4.3 %shard_map.57 = (bf16[1,192,768]{2,1,0:T(8,128)(2,1)}, f32[1,192,768]{2,1,0:T(8,128)}) custom-call(s32[2]{0:T(128)} %get-tuple-element.38.where_ref, bf16[384,3072]{1,0:T(8,128)(2,1)} %bitcast.17, bf16[384,1536]{1,0:T(8,128)(2,1)} %constant.80.clone.table_ref, bf16[2,8,192,1536]{3,2,1,0:T(8,128)(2,1)} %weight_ref.15), custom_call_target="tpu_custom_call" | custom-call | flops 452984832 | bytes 1179648 | tf_op jit(solution)/shard_map/pallas_call | solution.py:256
  100.3 0.5 collective-permute-start.1
  100.9 1.6 %collective-permute-start.4 = (bf16[1,192,768]{2,1,0:T(8,128)(2,1)S(1)}, bf16[1,192,768]{2,1,0:T(8,128)(2,1)S(1)}, u32[]{:S(2)}, u32[]{:S(2)}) collective-permute-start(bf16[1,192,768]{2,1,0:T(8,128)(2,1)S(1)} %add_convert_fusion.5), channel_id=1, source_target_pairs={{0,8},{4,12},{8,16},{12,20},{16,24},{20,28},{24,0},{28,4},{1,9},{5... | collective-permute-start | bytes 884744 | tf_op jit(solution)/shard_map/ppermute | solution.py:298
  102.6 2.6 %collective-permute-done.11 = bf16[1,192,768]{2,1,0:T(8,128)(2,1)S(1)} collective-permute-done((bf16[1,192,768]{2,1,0:T(8,128)(2,1)S(1)}, bf16[1,192,768]{2,1,0:T(8,128)(2,1)S(1)}, u32[]{:S(2)}, u32[]{:S(2)}) %collective-permute-start.11) | collective-permute-done | bytes 294944 | tf_op jit(solution)/shard_map/ppermute | solution.py:298
  105.2 0.1 add_convert_fusion.1
  105.3 4.4 %shard_map.60 = (bf16[1,192,768]{2,1,0:T(8,128)(2,1)}, f32[1,192,768]{2,1,0:T(8,128)}) custom-call(s32[2]{0:T(128)} %get-tuple-element.37.where_ref, bf16[384,3072]{1,0:T(8,128)(2,1)} %bitcast.18, bf16[384,1536]{1,0:T(8,128)(2,1)} %constant.80.clone.table_ref, bf16[2,8,192,1536]{3,2,1,0:T(8,128)(2,1)} %weight_ref.15), custom_call_target="tpu_custom_call" | custom-call | flops 452984832 | bytes 1179648 | tf_op jit(solution)/shard_map/pallas_call | solution.py:256
  109.7 0.5 collective-permute-start.7
  110.2 2.5 %collective-permute-done.4 = bf16[1,192,768]{2,1,0:T(8,128)(2,1)S(1)} collective-permute-done((bf16[1,192,768]{2,1,0:T(8,128)(2,1)S(1)}, bf16[1,192,768]{2,1,0:T(8,128)(2,1)S(1)}, u32[]{:S(2)}, u32[]{:S(2)}) %collective-permute-start.4) | collective-permute-done | bytes 294944 | tf_op jit(solution)/shard_map/ppermute | solution.py:298
  112.8 6.1 %collective-permute-done.12 = bf16[1,192,768]{2,1,0:T(8,128)(2,1)S(1)} collective-permute-done((bf16[1,192,768]{2,1,0:T(8,128)(2,1)S(1)}, bf16[1,192,768]{2,1,0:T(8,128)(2,1)S(1)}, u32[]{:S(2)}, u32[]{:S(2)}) %collective-permute-start.12) | collective-permute-done | bytes 294944 | tf_op jit(solution)/shard_map/ppermute | solution.py:298
  119.2 4.4 %shard_map.56 = (bf16[1,192,768]{2,1,0:T(8,128)(2,1)}, f32[1,192,768]{2,1,0:T(8,128)}) custom-call(s32[2]{0:T(128)} %get-tuple-element.37.where_ref, bf16[384,3072]{1,0:T(8,128)(2,1)} %bitcast.19, bf16[384,1536]{1,0:T(8,128)(2,1)} %constant.80.clone.table_ref, bf16[2,8,192,1536]{3,2,1,0:T(8,128)(2,1)} %weight_ref.15), custom_call_target="tpu_custom_call" | custom-call | flops 452984832 | bytes 1179648 | tf_op jit(solution)/shard_map/pallas_call | solution.py:256
  123.6 1.5 %collective-permute-start = (bf16[1,192,768]{2,1,0:T(8,128)(2,1)}, bf16[1,192,768]{2,1,0:T(8,128)(2,1)S(1)}, u32[]{:S(2)}, u32[]{:S(2)}) collective-permute-start(bf16[1,192,768]{2,1,0:T(8,128)(2,1)} %get-tuple-element.22), channel_id=1, source_target_pairs={{0,4},{4,0},{8,12},{12,8},{16,20},{20,16},{24,28},{28,24},{1,5},{5... | collective-permute-start | bytes 884744 | tf_op jit(solution)/shard_map/ppermute | solution.py:294
  125.1 0.2 collective-permute-done.5
  125.4 1.0 collective-permute-start.6
  126.4 5.2 %collective-permute-done.13 = bf16[1,192,768]{2,1,0:T(8,128)(2,1)S(1)} collective-permute-done((bf16[1,192,768]{2,1,0:T(8,128)(2,1)S(1)}, bf16[1,192,768]{2,1,0:T(8,128)(2,1)S(1)}, u32[]{:S(2)}, u32[]{:S(2)}) %collective-permute-start.13) | collective-permute-done | bytes 294944 | tf_op jit(solution)/shard_map/ppermute | solution.py:298
  131.7 4.6 %collective-permute-done.6 = bf16[1,192,768]{2,1,0:T(8,128)(2,1)S(1)} collective-permute-done((bf16[1,192,768]{2,1,0:T(8,128)(2,1)S(1)}, bf16[1,192,768]{2,1,0:T(8,128)(2,1)S(1)}, u32[]{:S(2)}, u32[]{:S(2)}) %collective-permute-start.6) | collective-permute-done | bytes 294944 | tf_op jit(solution)/shard_map/ppermute | solution.py:298
  136.4 1.2 maximum_multiply_fusion
  (35 shorter events, 0.8 us)
Async XLA Ops:
  71.1 23.2 %collective-permute-start.10 = (bf16[1,192,768]{2,1,0:T(8,128)(2,1)}, bf16[1,192,768]{2,1,0:T(8,128)(2,1)S(1)}, u32[]{:S(2)}, u32[]{:S(2)}) collective-permute-start(bf16[1,192,768]{2,1,0:T(8,128)(2,1)} %get-tuple-element.36), channel_id=1, source_target_pairs={{0,4},{4,0},{8,12},{12,8},{16,20},{20,16},{24,28},{28,24},{1,5},{5... | collective-permute-start | bytes 884744 | tf_op jit(solution)/shard_map/ppermute | solution.py:294
  76.8 23.5 %collective-permute-start.3 = (bf16[1,192,768]{2,1,0:T(8,128)(2,1)}, bf16[1,192,768]{2,1,0:T(8,128)(2,1)S(1)}, u32[]{:S(2)}, u32[]{:S(2)}) collective-permute-start(bf16[1,192,768]{2,1,0:T(8,128)(2,1)} %get-tuple-element.28), channel_id=1, source_target_pairs={{0,4},{4,0},{8,12},{12,8},{16,20},{20,16},{24,28},{28,24},{1,5},{5... | collective-permute-start | bytes 884744 | tf_op jit(solution)/shard_map/ppermute | solution.py:294
  81.6 19.3 %collective-permute-start.9 = (bf16[1,192,768]{2,1,0:T(8,128)(2,1)}, bf16[1,192,768]{2,1,0:T(8,128)(2,1)S(1)}, u32[]{:S(2)}, u32[]{:S(2)}) collective-permute-start(bf16[1,192,768]{2,1,0:T(8,128)(2,1)} %get-tuple-element.34), channel_id=1, source_target_pairs={{0,4},{4,0},{8,12},{12,8},{16,20},{20,16},{24,28},{28,24},{1,5},{5... | collective-permute-start | bytes 884744 | tf_op jit(solution)/shard_map/ppermute | solution.py:294
  87.3 22.4 %collective-permute-start.2 = (bf16[1,192,768]{2,1,0:T(8,128)(2,1)}, bf16[1,192,768]{2,1,0:T(8,128)(2,1)S(1)}, u32[]{:S(2)}, u32[]{:S(2)}) collective-permute-start(bf16[1,192,768]{2,1,0:T(8,128)(2,1)} %get-tuple-element.26), channel_id=1, source_target_pairs={{0,4},{4,0},{8,12},{12,8},{16,20},{20,16},{24,28},{28,24},{1,5},{5... | collective-permute-start | bytes 884744 | tf_op jit(solution)/shard_map/ppermute | solution.py:294
  88.5 5.9 %copy-start.3 = (f32[1,192,768]{2,1,0:T(8,128)S(1)}, f32[1,192,768]{2,1,0:T(8,128)}, u32[]{:S(2)}) copy-start(f32[1,192,768]{2,1,0:T(8,128)} %get-tuple-element.35) | copy-start | bytes 1769476
  92.8 20.0 %collective-permute-start.8 = (bf16[1,192,768]{2,1,0:T(8,128)(2,1)}, bf16[1,192,768]{2,1,0:T(8,128)(2,1)S(1)}, u32[]{:S(2)}, u32[]{:S(2)}) collective-permute-start(bf16[1,192,768]{2,1,0:T(8,128)(2,1)} %get-tuple-element.32), channel_id=1, source_target_pairs={{0,4},{4,0},{8,12},{12,8},{16,20},{20,16},{24,28},{28,24},{1,5},{5... | collective-permute-start | bytes 884744 | tf_op jit(solution)/shard_map/ppermute | solution.py:294
  94.4 6.5 %copy-start.2 = (f32[1,192,768]{2,1,0:T(8,128)S(1)}, f32[1,192,768]{2,1,0:T(8,128)}, u32[]{:S(2)}) copy-start(f32[1,192,768]{2,1,0:T(8,128)} %get-tuple-element.27) | copy-start | bytes 1769476
  94.4 10.7 %copy-start.5 = (f32[1,192,768]{2,1,0:T(8,128)S(1)}, f32[1,192,768]{2,1,0:T(8,128)}, u32[]{:S(2)}) copy-start(f32[1,192,768]{2,1,0:T(8,128)} %get-tuple-element.33) | copy-start | bytes 1769476
  94.4 10.7 %collective-permute-start.11 = (bf16[1,192,768]{2,1,0:T(8,128)(2,1)S(1)}, bf16[1,192,768]{2,1,0:T(8,128)(2,1)S(1)}, u32[]{:S(2)}, u32[]{:S(2)}) collective-permute-start(bf16[1,192,768]{2,1,0:T(8,128)(2,1)S(1)} %add_convert_fusion.2), channel_id=1, source_target_pairs={{0,8},{4,12},{8,16},{12,20},{16,24},{20,28},{24,0},{28,4},{1,9},{5... | collective-permute-start | bytes 884744 | tf_op jit(solution)/shard_map/ppermute | solution.py:298
  100.3 24.7 %collective-permute-start.1 = (bf16[1,192,768]{2,1,0:T(8,128)(2,1)}, bf16[1,192,768]{2,1,0:T(8,128)(2,1)S(1)}, u32[]{:S(2)}, u32[]{:S(2)}) collective-permute-start(bf16[1,192,768]{2,1,0:T(8,128)(2,1)} %get-tuple-element.24), channel_id=1, source_target_pairs={{0,4},{4,0},{8,12},{12,8},{16,20},{20,16},{24,28},{28,24},{1,5},{5... | collective-permute-start | bytes 884744 | tf_op jit(solution)/shard_map/ppermute | solution.py:294
  100.9 11.7 %collective-permute-start.4 = (bf16[1,192,768]{2,1,0:T(8,128)(2,1)S(1)}, bf16[1,192,768]{2,1,0:T(8,128)(2,1)S(1)}, u32[]{:S(2)}, u32[]{:S(2)}) collective-permute-start(bf16[1,192,768]{2,1,0:T(8,128)(2,1)S(1)} %add_convert_fusion.5), channel_id=1, source_target_pairs={{0,8},{4,12},{8,16},{12,20},{16,24},{20,28},{24,0},{28,4},{1,9},{5... | collective-permute-start | bytes 884744 | tf_op jit(solution)/shard_map/ppermute | solution.py:298
  105.2 13.7 %collective-permute-start.12 = (bf16[1,192,768]{2,1,0:T(8,128)(2,1)S(1)}, bf16[1,192,768]{2,1,0:T(8,128)(2,1)S(1)}, u32[]{:S(2)}, u32[]{:S(2)}) collective-permute-start(bf16[1,192,768]{2,1,0:T(8,128)(2,1)S(1)} %add_convert_fusion.1), channel_id=1, source_target_pairs={{0,8},{4,12},{8,16},{12,20},{16,24},{20,28},{24,0},{28,4},{1,9},{5... | collective-permute-start | bytes 884744 | tf_op jit(solution)/shard_map/ppermute | solution.py:298
  105.3 7.4 %copy-start.4 = (f32[1,192,768]{2,1,0:T(8,128)S(1)}, f32[1,192,768]{2,1,0:T(8,128)}, u32[]{:S(2)}) copy-start(f32[1,192,768]{2,1,0:T(8,128)} %get-tuple-element.25) | copy-start | bytes 1769476
  105.3 13.7 %copy-start.7 = (f32[1,192,768]{2,1,0:T(8,128)S(1)}, f32[1,192,768]{2,1,0:T(8,128)}, u32[]{:S(2)}) copy-start(f32[1,192,768]{2,1,0:T(8,128)} %get-tuple-element.31) | copy-start | bytes 1769476
  109.7 16.7 %collective-permute-start.7 = (bf16[1,192,768]{2,1,0:T(8,128)(2,1)}, bf16[1,192,768]{2,1,0:T(8,128)(2,1)S(1)}, u32[]{:S(2)}, u32[]{:S(2)}) collective-permute-start(bf16[1,192,768]{2,1,0:T(8,128)(2,1)} %get-tuple-element.30), channel_id=1, source_target_pairs={{0,4},{4,0},{8,12},{12,8},{16,20},{20,16},{24,28},{28,24},{1,5},{5... | collective-permute-start | bytes 884744 | tf_op jit(solution)/shard_map/ppermute | solution.py:294
  112.8 12.5 %collective-permute-start.5 = (bf16[1,192,768]{2,1,0:T(8,128)(2,1)S(1)}, bf16[1,192,768]{2,1,0:T(8,128)(2,1)S(1)}, u32[]{:S(2)}, u32[]{:S(2)}) collective-permute-start(bf16[1,192,768]{2,1,0:T(8,128)(2,1)S(1)} %add_convert_fusion.4), channel_id=1, source_target_pairs={{0,8},{4,12},{8,16},{12,20},{16,24},{20,28},{24,0},{28,4},{1,9},{5... | collective-permute-start | bytes 884744 | tf_op jit(solution)/shard_map/ppermute | solution.py:298
  119.1 6.2 %copy-start.6 = (f32[1,192,768]{2,1,0:T(8,128)S(1)}, f32[1,192,768]{2,1,0:T(8,128)}, u32[]{:S(2)}) copy-start(f32[1,192,768]{2,1,0:T(8,128)} %get-tuple-element.23) | copy-start | bytes 1769476
  119.1 12.5 %copy-start = (f32[1,192,768]{2,1,0:T(8,128)S(1)}, f32[1,192,768]{2,1,0:T(8,128)}, u32[]{:S(2)}) copy-start(f32[1,192,768]{2,1,0:T(8,128)} %get-tuple-element.29) | copy-start | bytes 1769476
  119.1 12.5 %collective-permute-start.13 = (bf16[1,192,768]{2,1,0:T(8,128)(2,1)S(1)}, bf16[1,192,768]{2,1,0:T(8,128)(2,1)S(1)}, u32[]{:S(2)}, u32[]{:S(2)}) collective-permute-start(bf16[1,192,768]{2,1,0:T(8,128)(2,1)S(1)} %add_convert_fusion), channel_id=1, source_target_pairs={{0,8},{4,12},{8,16},{12,20},{16,24},{20,28},{24,0},{28,4},{1,9},{5... | collective-permute-start | bytes 884744 | tf_op jit(solution)/shard_map/ppermute | solution.py:298
  123.6 12.8 %copy-start.1 = (f32[1,192,768]{2,1,0:T(8,128)S(1)}, f32[1,192,768]{2,1,0:T(8,128)}, u32[]{:S(2)}) copy-start(f32[1,192,768]{2,1,0:T(8,128)} %get-tuple-element.21) | copy-start | bytes 1769476
  123.6 8.1 %collective-permute-start = (bf16[1,192,768]{2,1,0:T(8,128)(2,1)}, bf16[1,192,768]{2,1,0:T(8,128)(2,1)S(1)}, u32[]{:S(2)}, u32[]{:S(2)}) collective-permute-start(bf16[1,192,768]{2,1,0:T(8,128)(2,1)} %get-tuple-element.22), channel_id=1, source_target_pairs={{0,4},{4,0},{8,12},{12,8},{16,20},{20,16},{24,28},{28,24},{1,5},{5... | collective-permute-start | bytes 884744 | tf_op jit(solution)/shard_map/ppermute | solution.py:294
  125.4 10.9 %collective-permute-start.6 = (bf16[1,192,768]{2,1,0:T(8,128)(2,1)S(1)}, bf16[1,192,768]{2,1,0:T(8,128)(2,1)S(1)}, u32[]{:S(2)}, u32[]{:S(2)}) collective-permute-start(bf16[1,192,768]{2,1,0:T(8,128)(2,1)S(1)} %add_convert_fusion.3), channel_id=1, source_target_pairs={{0,8},{4,12},{8,16},{12,20},{16,24},{20,28},{24,0},{28,4},{1,9},{5... | collective-permute-start | bytes 884744 | tf_op jit(solution)/shard_map/ppermute | solution.py:298
